TPU v7x, 512 devices: a whole 4x4x16 slice. The times are simulated.
512 devices in a mesh: cells: 64 (over x, z), feat: 8 (over y, core).
Axes of the slice: x: 4, y: 4, z: 16, core: 2. Of those that a mesh axis runs over, the one named last changes fastest.
Arguments:
- features: float32 [131072, 4096], P('cells', 'feat'), may hold values from -16 to 16
- labels: int32 [131072], P('cells'), may hold values from 0 to 7
- weights: float32 [8, 4096], P(None, 'feat'), may hold values from -0.09375 to 0.09375
Outputs:
- new_weights: float32 [8, 4096], P(None, 'feat')
- new_logits: float32 [8, 131072], P(None, 'cells')
All inputs are finite; a program needn't handle non-finite values.
Results may differ from a plain program's by a relative error of at most 0.00018.
Values sent between devices are 32-bit elements; how exact they have to be, the bound alone decides.
No kernel may reach another device: no remote copies, remote signals or barrier semaphores. Data moves between devices by JAX's collectives and lax.ppermute only.
A program may use at most 64 MiB of HBM per device.

v0:
```python
import jax
import jax.numpy as jnp
from jax import lax
from jax.sharding import PartitionSpec as P

ITERS = 2


HIGH = lax.Precision.HIGHEST
RIDGE = 0.01


def copy_for_each(array, axis):
    devices = lax.axis_size(axis)
    return lax.all_to_all(
        jnp.broadcast_to(array[None], (devices, *array.shape)), axis, 0, 0, tiled=True
    )


def of_everyone(array, axis):
    return copy_for_each(array, axis).sum(axis=0)


def on_device(features, labels, weights):
    rows = features.shape[0]
    classes = weights.shape[0]
    count = rows * lax.axis_size("cells") * 1.0

    def row_sums(coeffs, extra):
        local_rows = lax.dot_general(
            coeffs,
            features,
            (((1,), (1,)), ((), ())),
            precision=HIGH,
            preferred_element_type=jnp.float32,
        )
        stacked = local_rows if extra is None else jnp.concatenate([local_rows, extra], axis=0)
        summed = of_everyone(stacked, "feat")
        return (summed[:classes], summed[classes:])

    def collect(terms):
        return of_everyone(jnp.dot(terms, features, precision=HIGH), "cells")

    logits, unused = row_sums(weights, None)
    expo = jnp.exp(logits)
    probs = expo / jnp.sum(expo, axis=0, keepdims=True)
    onehot = (labels[None, :] == jnp.arange(classes, dtype=jnp.int32)[:, None]).astype(jnp.float32)
    grad = collect(probs - onehot) / count + RIDGE * weights
    resid = -grad
    direction = resid
    rr_now = jnp.float32(0.0)
    step = jnp.zeros_like(weights)
    moved = jnp.zeros_like(logits)
    for it in range(ITERS):
        full_direction = direction
        if it == 0:
            partial_value = jnp.sum(full_direction * full_direction)
            column = lax.broadcasted_iota(jnp.int32, (1, rows), 1)
            extra = jnp.where(column == 0, partial_value, jnp.float32(0.0))
            image, tail = row_sums(full_direction, extra)
            rr_now = tail[0, 0]
        else:
            image, unused = row_sums(full_direction, None)
        curv = probs * image - probs * jnp.sum(probs * image, axis=0, keepdims=True)
        product = collect(curv) / count + RIDGE * direction
        triple_packed = jnp.stack(
            [jnp.sum(direction * product), jnp.sum(resid * product), jnp.sum(product * product)]
        )
        triple_summed = of_everyone(triple_packed, "feat")
        along = triple_summed[0]
        cross = triple_summed[1]
        square = triple_summed[2]
        alpha = rr_now / along
        step = step + alpha * direction
        moved = moved + alpha * image
        resid = resid - alpha * product
        if it + 1 < ITERS:
            rr_next = rr_now - 2.0 * alpha * cross + alpha * alpha * square
            direction = resid + rr_next / rr_now * direction
            rr_now = rr_next
    return (weights + step, logits + moved)


def solution(mesh):
    return jax.shard_map(
        on_device,
        mesh=mesh,
        in_specs=(P("cells", "feat"), P("cells"), P(None, "feat")),
        out_specs=(P(None, "feat"), P(None, "cells")),
        check_vma=False,
    )
```

profile of v0, /device:TPU:1, one launch (start us, length us, event | category | flops | bytes accessed | tf_op | source)
XLA Modules:
  0.0 299.2 jit_solution(15719831702337004577)
XLA Ops:
  0.6 0.0 copy-start.1
  0.6 5.7 %fusion.20 = f32[8,2048]{1,0:T(8,128)S(1)} fusion(f32[8,512]{1,0:T(8,128)} %param.5, f32[2048,512]{1,0:T(8,128)} %param.3), kind=kOutput, calls=%fused_computation.40 | convolution fusion | flops 100663296 | bytes 4276224 | tf_op jit(solution)/shard_map/dot_general | solution.py:30
  6.4 18.6 %all_to_all.42 = f32[8,8,2048]{2,1,0:T(8,128)S(1)} all-to-all(f32[8,8,2048]{2,1,0:T(8,128)S(1)} %broadcast_in_dim.24), channel_id=1, replica_groups=mesh['cells'=64,'feat'=8] {'feat'}, dimensions={0} | all-to-all | bytes 1048576 | tf_op jit(solution)/shard_map/all_to_all | solution.py:15
  25.0 0.0 copy-done.1
  25.0 0.0 copy-start
  25.0 4.3 %fusion.6 = f32[8,512]{1,0:T(8,128)S(1)} fusion(f32[2048,512]{1,0:T(8,128)} %param.3, s32[2048]{0:T(1024)S(1)} %copy-done.1, f32[8,2048]{1,0:T(8,128)S(1)} %reduce_sum.157, f32[2048]{0:T(1024)S(1)} %exponential_reduce_fusion), kind=kOutput, calls=%fused_computation.8 | convolution fusion | flops 100728832 | bytes 4292608 | tf_op jit(solution)/shard_map/dot_general | solution.py:42
  29.3 0.1 broadcast_in_dim.25
  29.4 64.8 %all_to_all.43 = f32[64,8,512]{2,1,0:T(8,128)S(1)} all-to-all(f32[64,8,512]{2,1,0:T(8,128)S(1)} %broadcast_in_dim.25), channel_id=1, replica_groups=mesh['cells'=64,'feat'=8] {'cells'}, dimensions={0} | all-to-all | bytes 2097152 | tf_op jit(solution)/shard_map/all_to_all | solution.py:15
  94.2 0.1 reduce_sum.159
  94.3 0.0 copy-done
  94.3 0.6 multiply_reduce_fusion.5
  94.9 0.6 compare_select_fusion
  95.6 5.7 %fusion.13 = f32[8,2048]{1,0:T(8,128)S(1)} fusion(f32[2048,512]{1,0:T(8,128)} %param.3, f32[8,512]{1,0:T(8,128)S(1)} %get-tuple-element.8), kind=kOutput, calls=%fused_computation.32 | convolution fusion | flops 100667392 | bytes 4276224 | tf_op jit(solution)/shard_map/dot_general | solution.py:30
  101.3 0.1 broadcast_in_dim.28
  101.4 22.0 %all_to_all.44 = f32[8,9,2048]{2,1,0:T(8,128)S(1)} all-to-all(f32[8,9,2048]{2,1,0:T(8,128)S(1)} %broadcast_in_dim.28), channel_id=1, replica_groups=mesh['cells'=64,'feat'=8] {'feat'}, dimensions={0} | all-to-all | bytes 1179648 | tf_op jit(solution)/shard_map/all_to_all | solution.py:15
  123.4 0.1 reduce_sum.161
  123.5 4.3 %fusion.3 = f32[8,512]{1,0:T(8,128)S(1)} fusion(f32[2048,512]{1,0:T(8,128)} %param.3, f32[9,2048]{1,0:T(8,128)S(1)} %reduce_sum.161, f32[2048]{0:T(1024)S(1)} %fusion.9, f32[8,2048]{1,0:T(8,128)S(1)} %reduce_sum.157, f32[2048]{0:T(1024)S(1)} %exponential_reduce_fusion), kind=kOutput, calls=%fused_computation.5 | convolution fusion | flops 100728832 | bytes 4358144 | tf_op jit(solution)/shard_map/dot_general | solution.py:42
  127.8 0.1 broadcast_in_dim.29
  127.9 56.6 %all_to_all.45 = f32[64,8,512]{2,1,0:T(8,128)S(1)} all-to-all(f32[64,8,512]{2,1,0:T(8,128)S(1)} %broadcast_in_dim.29), channel_id=1, replica_groups=mesh['cells'=64,'feat'=8] {'cells'}, dimensions={0} | all-to-all | bytes 2097152 | tf_op jit(solution)/shard_map/all_to_all | solution.py:15
  184.5 0.1 reduce_sum.163
  184.6 0.6 multiply_reduce_fusion.4
  185.2 1.4 pad_maximum_fusion.1
  186.6 0.6 broadcast_in_dim.30
  187.2 7.9 %all-to-all-start.4 = ((f32[8,1,3]{2,1,0:T(1,128)}), f32[8,1,3]{2,1,0:T(1,128)S(1)}, u32[]{:S(2)}, u32[]{:S(2)}) async-start(f32[8,1,3]{2,1,0:T(1,128)} %broadcast_in_dim.30), calls=%async_computation.4 | async-start | bytes 8192 | tf_op jit(solution)/shard_map/all_to_all | solution.py:15
  195.1 0.5 slice.26
  195.6 4.0 %all-to-all-done.4 = f32[8,1,3]{2,1,0:T(1,128)S(1)} async-done(((f32[8,1,3]{2,1,0:T(1,128)}), f32[8,1,3]{2,1,0:T(1,128)S(1)}, u32[]{:S(2)}, u32[]{:S(2)}) %all-to-all-start.4) | async-done | bytes 128 | tf_op jit(solution)/shard_map/all_to_all | solution.py:15
  199.7 0.7 fusion.19
  204.2 5.7 %fusion.15 = f32[8,2048]{1,0:T(8,128)S(1)} fusion(f32[2048,512]{1,0:T(8,128)} %param.3, f32[8,512]{1,0:T(8,128)S(1)} %get-tuple-element.8, f32[]{:T(128)S(6)} %div.31, f32[]{:T(128)S(6)} %div.30, f32[8,512]{1,0:T(8,128)S(1)} %reduce_sum.163), kind=kOutput, calls=%fused_computation.36 | convolution fusion | flops 100696064 | bytes 4292616 | tf_op jit(solution)/shard_map/dot_general | solution.py:30
  210.0 12.4 %all_to_all.46 = f32[8,8,2048]{2,1,0:T(8,128)S(1)} all-to-all(f32[8,8,2048]{2,1,0:T(8,128)S(1)} %broadcast_in_dim.31), channel_id=1, replica_groups=mesh['cells'=64,'feat'=8] {'feat'}, dimensions={0} | all-to-all | bytes 1048576 | tf_op jit(solution)/shard_map/all_to_all | solution.py:15
  222.5 4.3 %fusion = f32[8,512]{1,0:T(8,128)S(1)} fusion(f32[2048,512]{1,0:T(8,128)} %param.3, f32[2048]{0:T(1024)S(1)} %fusion.18, f32[8,2048]{1,0:T(8,128)S(1)} %reduce_sum.157, f32[2048]{0:T(1024)S(1)} %exponential_reduce_fusion, f32[8,2048]{1,0:T(8,128)S(1)} %reduce_sum.167), kind=kOutput, calls=%fused_computation.2 | convolution fusion | flops 100728832 | bytes 4358144 | tf_op jit(solution)/shard_map/dot_general | solution.py:42
  226.7 0.1 broadcast_in_dim.32
  226.9 56.4 %all_to_all.47 = f32[64,8,512]{2,1,0:T(8,128)S(1)} all-to-all(f32[64,8,512]{2,1,0:T(8,128)S(1)} %broadcast_in_dim.32), channel_id=1, replica_groups=mesh['cells'=64,'feat'=8] {'cells'}, dimensions={0} | all-to-all | bytes 2097152 | tf_op jit(solution)/shard_map/all_to_all | solution.py:15
  283.3 0.1 reduce_sum.169
  283.4 0.7 multiply_reduce_fusion.2
  284.1 2.1 pad_maximum_fusion.2
  286.2 11.6 %all_to_all.48 = f32[8,1,3]{2,1,0:T(1,128)S(1)} all-to-all(f32[8,1,3]{2,1,0:T(1,128)S(1)} %broadcast_in_dim.33), channel_id=1, replica_groups=mesh['cells'=64,'feat'=8] {'feat'}, dimensions={0} | all-to-all | bytes 192 | tf_op jit(solution)/shard_map/all_to_all | solution.py:15
  297.9 0.6 add_add_fusion
  298.5 0.6 add_add_fusion.1
  (11 shorter events, 0.3 us)
Async XLA Ops:
  0.6 24.4 %copy-start.1 = (s32[2048]{0:T(1024)S(1)}, s32[2048]{0:T(1024)}, u32[]{:S(2)}) copy-start(s32[2048]{0:T(1024)} %param.4) | copy-start | bytes 24580
  25.0 69.3 %copy-start = (f32[8,512]{1,0:T(8,128)S(1)}, f32[8,512]{1,0:T(8,128)}, u32[]{:S(2)}) copy-start(f32[8,512]{1,0:T(8,128)} %param.5) | copy-start | bytes 49156
  187.2 12.4 %all-to-all-start.4 = ((f32[8,1,3]{2,1,0:T(1,128)}), f32[8,1,3]{2,1,0:T(1,128)S(1)}, u32[]{:S(2)}, u32[]{:S(2)}) async-start(f32[8,1,3]{2,1,0:T(1,128)} %broadcast_in_dim.30), calls=%async_computation.4 | async-start | bytes 8192 | tf_op jit(solution)/shard_map/all_to_all | solution.py:15
where the time goes:
time: 300 us; the launch traced here: 299 us
  blocking collectives  242 us (81%)
  matrix products  29.8 us (10%)
  starting transfers between devices  7.89 us (3%)
  other arithmetic  7.84 us (3%)
  between operations  4.78 us (2%)
  waiting for transfers between devices  4.03 us (1%)
    all_to_all x7, blocking collectives, copy_for_each(): lax.all_to_all(jnp.broadcast_to(array[None], (devices, *array.shape)), ax...  242 us
    dot_general x3, matrix products, row_sums(): lax.dot_general(coeffs, features, (((1,), (1,)), ((), ())), precision=HIG...  17 us
    dot_general x3, matrix products, collect(): return of_everyone(jnp.dot(terms, features, precision=HIGH), 'cells')  12.8 us
    all_to_all x1, starting transfers between devices, copy_for_each(): lax.all_to_all(jnp.broadcast_to(array[None], (devices, *array.shape)), ax...  7.89 us
  transfers between devices with their start and end apart: 1, of which 1 were waited for; matrix products, arithmetic and copies ran while one was open for 0% of the time, Pallas kernels for 0%

commit v1 on v0

v1 whole, which is shorter than its diff:
```python
import jax
import jax.numpy as jnp
from jax import lax
from jax.sharding import Mesh, PartitionSpec as P

HIGH = lax.Precision.HIGH
RIDGE = 0.01
CELLS = ("x", "z")
FEAT = ("y", "core")


def from_everyone(array, axes):
    devices = lax.axis_size(axes)
    return lax.all_to_all(
        jnp.broadcast_to(array[None], (devices, *array.shape)), axes, 0, 0, tiled=True
    )


def on_device(features, labels, weights):
    rows = features.shape[0]
    classes, width = weights.shape
    count = rows * lax.axis_size(CELLS) * 1.0
    planes = lax.axis_size("x")

    def row_sums(coeffs):
        return lax.dot_general(
            coeffs, features, (((1,), (1,)), ((), ())), precision=HIGH, preferred_element_type=jnp.float32
        )

    def over_feat(local_rows):
        return from_everyone(local_rows, FEAT).sum(axis=0)

    def over_cells(terms):
        local = jnp.dot(terms, features, precision=HIGH, preferred_element_type=jnp.float32)
        blocks = local.reshape(classes, planes, width // planes).transpose(1, 0, 2)
        block = lax.all_to_all(blocks, "x", 0, 0, tiled=True).sum(axis=0)
        block = from_everyone(block, "z").sum(axis=0)
        blocks = from_everyone(block, "x")
        return blocks.transpose(1, 0, 2).reshape(classes, width)

    def with_sums(local_rows, first, second):
        column = lax.broadcasted_iota(jnp.int32, (classes, 128), 1)
        tail = jnp.where(column == 0, first, jnp.where(column == 1, second, jnp.float32(0.0)))
        summed = over_feat(jnp.concatenate([local_rows, tail], axis=1))
        return summed[:, :rows], summed[0, rows], summed[0, rows + 1]

    logits = over_feat(row_sums(weights))
    expo = jnp.exp(logits)
    probs = expo / jnp.sum(expo, axis=0, keepdims=True)
    onehot = (labels[None, :] == jnp.arange(classes, dtype=jnp.int32)[:, None]).astype(jnp.float32)
    resid = -(over_cells(probs - onehot) / count + RIDGE * weights)

    def curved(image):
        return probs * image - probs * jnp.sum(probs * image, axis=0, keepdims=True)

    image, rr0, unused = with_sums(row_sums(resid), jnp.sum(resid * resid), jnp.float32(0.0))
    product = over_cells(curved(image)) / count + RIDGE * resid
    product_image, along, square = with_sums(
        row_sums(product), jnp.sum(resid * product), jnp.sum(product * product)
    )
    alpha0 = rr0 / along
    rr1 = rr0 - 2.0 * alpha0 * along + alpha0 * alpha0 * square
    beta = rr1 / rr0
    direction = resid - alpha0 * product + beta * resid
    direction_image = image - alpha0 * product_image + beta * image
    curvature = jnp.sum(direction_image * curved(direction_image))
    curvature = from_everyone(jnp.full((1, 128), curvature), CELLS)[:, :, :1].sum()
    alpha1 = rr1 / (curvature / count + RIDGE * (rr1 + beta * beta * rr0))
    return (
        weights + (alpha0 * resid + alpha1 * direction),
        logits + (alpha0 * image + alpha1 * direction_image),
    )


def solution(mesh):
    grid = Mesh(mesh.devices.reshape(4, 16, 4, 2), CELLS + FEAT)
    return jax.shard_map(
        on_device,
        mesh=grid,
        in_specs=(P(CELLS, FEAT), P(CELLS), P(None, FEAT)),
        out_specs=(P(None, FEAT), P(None, CELLS)),
        check_vma=False,
    )
```

time: 300 us -> 171 us (0.57)
  blocking collectives: 242 us -> 94.5 us
  waiting for transfers between devices: 4.03 us -> 26 us
  matrix products: 29.8 us -> 18.4 us
  starting transfers between devices: 7.89 us -> 15.4 us
    all_to_all x7, blocking collectives: 242 us -> 94.5 us  [the longest x5 81.4 us: from_everyone(): lax.all_to_all(jnp.broadcast_to(array[None], (devices, *array.shape)), ax...]
    all_to_all x1 -> x3, waiting for transfers between devices: 4.03 us -> 26 us  [from_everyone(): lax.all_to_all(jnp.broadcast_to(array[None], (devices, *array.shape)), ax...]
    all_to_all x1 -> x3, starting transfers between devices: 7.89 us -> 15.4 us  [from_everyone(): lax.all_to_all(jnp.broadcast_to(array[None], (devices, *array.shape)), ax...]
    dot_general x3 -> x2, matrix products: 12.8 us -> 6.65 us  [over_cells(): jnp.dot(terms, features, precision=HIGH, preferred_element_type=jnp.float32)]
    dot_general x3, matrix products: 17 us -> 11.8 us  [row_sums(): lax.dot_general(coeffs, features, (((1,), (1,)), ((), ())), precision=HIG...]
    another operation x2 -> x0, other arithmetic: 3.42 us -> none  [on_device(): jnp.stack([jnp.sum(direction * product), jnp.sum(resid * product), jnp.su...]
  transfers between devices with their start and end apart: 1 -> 3, of which waited for: 1 -> 3; matrix products, arithmetic and copies ran while one was open for 0% -> 0% of each run, Pallas kernels for 0% -> 0%
where the time goes in v1:
time: 171 us
  blocking collectives  94.5 us (55%)
  waiting for transfers between devices  26 us (15%)
  matrix products  18.4 us (11%)
  starting transfers between devices  15.4 us (9%)
  between operations  6.18 us (4%)
  other arithmetic  6.1 us (4%)
  local copies, waits for them, and re-layouts  3.98 us (2%)
    all_to_all x5, blocking collectives, from_everyone(): lax.all_to_all(jnp.broadcast_to(array[None], (devices, *array.shape)), ax...  81.4 us
    all_to_all x3, waiting for transfers between devices, from_everyone(): lax.all_to_all(jnp.broadcast_to(array[None], (devices, *array.shape)), ax...  26 us
    all_to_all x3, starting transfers between devices, from_everyone(): lax.all_to_all(jnp.broadcast_to(array[None], (devices, *array.shape)), ax...  15.4 us
    all_to_all x2, blocking collectives, over_cells(): block = lax.all_to_all(blocks, 'x', 0, 0, tiled=True).sum(axis=0)  13.1 us
    dot_general x3, matrix products, row_sums(): lax.dot_general(coeffs, features, (((1,), (1,)), ((), ())), precision=HIG...  11.8 us
    dot_general x2, matrix products, over_cells(): jnp.dot(terms, features, precision=HIGH, preferred_element_type=jnp.float32)  6.65 us
  transfers between devices with their start and end apart: 3, of which 3 were waited for; matrix products, arithmetic and copies ran while one was open for 0% of the time, Pallas kernels for 0%

profile of v1, /device:TPU:1, one launch (start us, length us, event | category | flops | bytes accessed | tf_op | source)
XLA Modules:
  0.0 170.5 jit_solution(15945304551709702726)
XLA Ops:
  0.6 0.0 copy-start.1
  0.6 3.9 %fusion.16 = f32[8,2048]{1,0:T(8,128)S(1)} fusion(f32[8,512]{1,0:T(8,128)} %param.5, f32[2048,512]{1,0:T(8,128)} %param.3), kind=kOutput, calls=%fused_computation.37 | convolution fusion | flops 50331648 | bytes 4276224 | tf_op jit(solution)/shard_map/dot_general | solution.py:26
  4.6 0.0 copy-start
  4.6 18.6 %all_to_all.50 = f32[8,8,2048]{2,1,0:T(8,128)S(1)} all-to-all(f32[8,8,2048]{2,1,0:T(8,128)S(1)} %broadcast_in_dim.29), channel_id=1, replica_groups=mesh['x'=4,'z'=16,'y'=4,'core'=2] {'y','core'}, dimensions={0} | all-to-all | bytes 1048576 | tf_op jit(solution)/shard_map/all_to_all | solution.py:14
  23.3 0.0 copy-done.1
  23.3 3.3 %convolution_bitcast_fusion.1 = f32[4,8,128]{2,1,0:T(8,128)S(1)} fusion(f32[2048,512]{1,0:T(8,128)} %param.3, s32[2048]{0:T(1024)S(1)} %copy-done.1, f32[8,2048]{1,0:T(8,128)S(1)} %reduce_sum.135, f32[2048]{0:T(1024)S(1)} %exponential_reduce_fusion), kind=kOutput, calls=%fused_computation.1 | convolution fusion | flops 50397184 | bytes 4292608 | tf_op jit(solution)/shard_map/dot_general | solution.py:34
  26.6 6.6 %all_to_all.51 = f32[4,8,128]{2,1,0:T(8,128)S(1)} all-to-all(f32[4,8,128]{2,1,0:T(8,128)S(1)} %convolution_bitcast_fusion.1), channel_id=1, replica_groups=mesh['x'=4,'z'=16,'y'=4,'core'=2] {'x'}, dimensions={0} | all-to-all | bytes 32768 | tf_op jit(solution)/shard_map/all_to_all | solution.py:36
  33.2 24.3 %all_to_all.52 = f32[16,8,128]{2,1,0:T(8,128)S(1)} all-to-all(f32[16,8,128]{2,1,0:T(8,128)S(1)} %broadcast_in_dim.30), channel_id=1, replica_groups=mesh['x'=4,'z'=16,'y'=4,'core'=2] {'z'}, dimensions={0} | all-to-all | bytes 131072 | tf_op jit(solution)/shard_map/all_to_all | solution.py:14
  57.5 6.6 %all_to_all.53 = f32[4,8,128]{2,1,0:T(8,128)S(1)} all-to-all(f32[4,8,128]{2,1,0:T(8,128)S(1)} %broadcast_in_dim.31), channel_id=1, replica_groups=mesh['x'=4,'z'=16,'y'=4,'core'=2] {'x'}, dimensions={0} | all-to-all | bytes 32768 | tf_op jit(solution)/shard_map/all_to_all | solution.py:14
  64.0 0.0 copy-done
  64.0 0.6 multiply_reduce_fusion.3
  64.6 3.9 %fusion.9 = f32[8,2048]{1,0:T(8,128)S(1)} fusion(f32[2048,512]{1,0:T(8,128)} %param.3, f32[8,512]{1,0:T(8,128)S(1)} %get-tuple-element.7), kind=kOutput, calls=%fused_computation.27 | convolution fusion | flops 50335744 | bytes 4276224 | tf_op jit(solution)/shard_map/dot_general | solution.py:26
  68.5 0.7 broadcast_select_fusion.1
  69.3 17.7 %all_to_all.54 = f32[8,8,2176]{2,1,0:T(8,128)S(1)} all-to-all(f32[8,8,2176]{2,1,0:T(8,128)S(1)} %broadcast_in_dim.33), channel_id=1, replica_groups=mesh['x'=4,'z'=16,'y'=4,'core'=2] {'y','core'}, dimensions={0} | all-to-all | bytes 1114112 | tf_op jit(solution)/shard_map/all_to_all | solution.py:14
  87.1 3.3 %convolution_bitcast_fusion = f32[4,8,128]{2,1,0:T(8,128)S(1)} fusion(f32[2048,512]{1,0:T(8,128)} %param.3, f32[8,2176]{1,0:T(8,128)S(1)} %reduce_sum.140, f32[2048]{0:T(1024)S(1)} %fusion.6, f32[8,2048]{1,0:T(8,128)S(1)} %reduce_sum.135, f32[2048]{0:T(1024)S(1)} %exponential_reduce_fusion), kind=kOutput, calls=%fused_computation | convolution fusion | flops 50397184 | bytes 4358144 | tf_op jit(solution)/shard_map/dot_general | solution.py:34
  90.4 6.6 %all_to_all.55 = f32[4,8,128]{2,1,0:T(8,128)S(1)} all-to-all(f32[4,8,128]{2,1,0:T(8,128)S(1)} %convolution_bitcast_fusion), channel_id=1, replica_groups=mesh['x'=4,'z'=16,'y'=4,'core'=2] {'x'}, dimensions={0} | all-to-all | bytes 32768 | tf_op jit(solution)/shard_map/all_to_all | solution.py:36
  97.0 14.2 %all_to_all.56 = f32[16,8,128]{2,1,0:T(8,128)S(1)} all-to-all(f32[16,8,128]{2,1,0:T(8,128)S(1)} %broadcast_in_dim.34), channel_id=1, replica_groups=mesh['x'=4,'z'=16,'y'=4,'core'=2] {'z'}, dimensions={0} | all-to-all | bytes 131072 | tf_op jit(solution)/shard_map/all_to_all | solution.py:14
  111.3 0.6 broadcast_in_dim.35
  111.9 3.3 %all-to-all-start.7 = ((f32[4,8,128]{2,1,0:T(8,128)}), f32[4,8,128]{2,1,0:T(8,128)S(1)}, u32[]{:S(2)}, u32[]{:S(2)}) async-start(f32[4,8,128]{2,1,0:T(8,128)} %broadcast_in_dim.35), calls=%async_computation.7 | async-start | bytes 32768 | tf_op jit(solution)/shard_map/all_to_all | solution.py:14
  115.1 4.2 %all-to-all-done.7 = f32[4,8,128]{2,1,0:T(8,128)S(1)} async-done(((f32[4,8,128]{2,1,0:T(8,128)}), f32[4,8,128]{2,1,0:T(8,128)S(1)}, u32[]{:S(2)}, u32[]{:S(2)}) %all-to-all-start.7) | async-done | bytes 16416 | tf_op jit(solution)/shard_map/all_to_all | solution.py:14
  119.3 0.6 multiply_reduce_fusion.2
  119.9 0.6 compare_select_fusion
  120.6 0.7 broadcast_select_fusion
  121.2 3.9 %fusion.11 = f32[8,2048]{1,0:T(8,128)S(1)} fusion(f32[2048,512]{1,0:T(8,128)} %param.3, f32[4,8,128]{2,1,0:T(8,128)S(1)} %all-to-all-done.7, f32[8,512]{1,0:T(8,128)S(1)} %get-tuple-element.7), kind=kOutput, calls=%fused_computation.33 | convolution fusion | flops 50348032 | bytes 4292608 | tf_op jit(solution)/shard_map/dot_general | solution.py:26
  125.2 0.8 broadcast_in_dim.38
  126.0 7.6 %all-to-all-start.8 = ((f32[8,8,2176]{2,1,0:T(8,128)}), f32[8,8,2176]{2,1,0:T(8,128)S(1)}, u32[]{:S(2)}, u32[]{:S(2)}) async-start(f32[8,8,2176]{2,1,0:T(8,128)} %broadcast_in_dim.38), calls=%async_computation.8 | async-start | bytes 1114112 | tf_op jit(solution)/shard_map/all_to_all | solution.py:14
  133.6 0.5 slice.24
  134.1 9.2 %all-to-all-done.8 = f32[8,8,2176]{2,1,0:T(8,128)S(1)} async-done(((f32[8,8,2176]{2,1,0:T(8,128)}), f32[8,8,2176]{2,1,0:T(8,128)S(1)}, u32[]{:S(2)}, u32[]{:S(2)}) %all-to-all-start.8) | async-done | bytes 557088 | tf_op jit(solution)/shard_map/all_to_all | solution.py:14
  143.3 0.6 fusion.15
  148.0 0.7 multiply_reduce_fusion
  148.8 1.3 broadcast_in_dim_broadcast_in_dim_broadcast_in_dim.3
  150.1 4.6 %all-to-all-start.9 = ((f32[64,1,128]{2,1,0:T(1,128)}), f32[64,1,128]{2,1,0:T(1,128)S(1)}, u32[]{:S(2)}, u32[]{:S(2)}) async-start(f32[64,1,128]{2,1,0:T(1,128)} %broadcast_in_dim_broadcast_in_dim_broadcast_in_dim.3), calls=%async_computation.9 | async-start | bytes 65536 | tf_op jit(solution)/shard_map/all_to_all | solution.py:14
  155.3 12.6 %all-to-all-done.9 = f32[64,1,128]{2,1,0:T(1,128)S(1)} async-done(((f32[64,1,128]{2,1,0:T(1,128)}), f32[64,1,128]{2,1,0:T(1,128)S(1)}, u32[]{:S(2)}, u32[]{:S(2)}) %all-to-all-start.9) | async-done | bytes 32800 | tf_op jit(solution)/shard_map/all_to_all | solution.py:14
  167.9 0.7 slice_reduce_fusion
  169.3 0.6 add_add_fusion
  169.9 0.6 add_add_fusion.1
  (19 shorter events, 0.4 us)
Async XLA Ops:
  0.6 22.6 %copy-start.1 = (s32[2048]{0:T(1024)S(1)}, s32[2048]{0:T(1024)}, u32[]{:S(2)}) copy-start(s32[2048]{0:T(1024)} %param.4) | copy-start | bytes 24580
  4.6 59.5 %copy-start = (f32[8,512]{1,0:T(8,128)S(1)}, f32[8,512]{1,0:T(8,128)}, u32[]{:S(2)}) copy-start(f32[8,512]{1,0:T(8,128)} %param.5) | copy-start | bytes 49156
  111.9 7.4 %all-to-all-start.7 = ((f32[4,8,128]{2,1,0:T(8,128)}), f32[4,8,128]{2,1,0:T(8,128)S(1)}, u32[]{:S(2)}, u32[]{:S(2)}) async-start(f32[4,8,128]{2,1,0:T(8,128)} %broadcast_in_dim.35), calls=%async_computation.7 | async-start | bytes 32768 | tf_op jit(solution)/shard_map/all_to_all | solution.py:14
  126.0 17.3 %all-to-all-start.8 = ((f32[8,8,2176]{2,1,0:T(8,128)}), f32[8,8,2176]{2,1,0:T(8,128)S(1)}, u32[]{:S(2)}, u32[]{:S(2)}) async-start(f32[8,8,2176]{2,1,0:T(8,128)} %broadcast_in_dim.38), calls=%async_computation.8 | async-start | bytes 1114112 | tf_op jit(solution)/shard_map/all_to_all | solution.py:14
  150.1 17.8 %all-to-all-start.9 = ((f32[64,1,128]{2,1,0:T(1,128)}), f32[64,1,128]{2,1,0:T(1,128)S(1)}, u32[]{:S(2)}, u32[]{:S(2)}) async-start(f32[64,1,128]{2,1,0:T(1,128)} %broadcast_in_dim_broadcast_in_dim_broadcast_in_dim.3), calls=%async_computation.9 | async-start | bytes 65536 | tf_op jit(solution)/shard_map/all_to_all | solution.py:14

commit v2 on v1

v2 whole, which is shorter than its diff:
```python
import functools

import jax
import jax.numpy as jnp
from jax import lax
from jax.experimental import pallas as pl
from jax.experimental.pallas import tpu as pltpu
from jax.sharding import Mesh, PartitionSpec as P

RIDGE = 0.01
CELLS = ("x", "z")
FEAT = ("y", "core")
LANES = 128
CHUNK = 256
F32 = jnp.float32
BF16 = jnp.bfloat16
NN = (((1,), (0,)), ((), ()))
NT = (((1,), (1,)), ((), ()))


def both_parts(value):
    high = value.astype(BF16).astype(F32)
    return jnp.concatenate([high, value - high], axis=0).astype(BF16)


def product_of(parts, high, low, dims):
    k = parts.shape[0] // 2
    one = lax.dot_general(parts, high, dims, preferred_element_type=F32)
    two = lax.dot_general(parts, low, dims, preferred_element_type=F32)
    total = one + two
    return total[:k] + total[k:]


def sum_first(ref, lo=None, hi=None):
    total = ref[0] if lo is None else ref[0, :, lo:hi]
    for i in range(1, ref.shape[0]):
        total = total + (ref[i] if lo is None else ref[i, :, lo:hi])
    return total


def curved(probs, image):
    weighted = probs * image
    return weighted - probs * jnp.sum(weighted, axis=0, keepdims=True)


def total_of(value):
    return jnp.sum(jnp.sum(value, axis=1, keepdims=True), axis=0, keepdims=True)


def tile_of(first, second):
    column = lax.broadcasted_iota(jnp.int32, (8, LANES), 1)
    return jnp.where(column == 0, first, jnp.where(column == 1, second, 0.0))


def spread(ref, value, cols=slice(None)):
    for i in range(ref.shape[0]):
        ref[i, :, cols] = value


def relay_kernel(recv_ref, out_ref):
    spread(out_ref, sum_first(recv_ref))


def first_kernel(w_ref, x_ref, high_ref, low_ref, out_ref, held_w, held, sems):
    steps = held.shape[0] // CHUNK
    copies = []
    weights = pltpu.make_async_copy(w_ref, held_w, sems.at[steps])
    weights.start()
    for i in range(steps):
        rows = pl.ds(i * CHUNK, CHUNK)
        copy = pltpu.make_async_copy(x_ref.at[rows], held.at[rows], sems.at[i])
        copy.start()
        copies.append(copy)
    weights.wait()
    parts = both_parts(held_w[...])
    for i in range(steps):
        rows = pl.ds(i * CHUNK, CHUNK)
        copies[i].wait()
        x = held[rows, :]
        high = x.astype(BF16)
        low = (x - high.astype(F32)).astype(BF16)
        high_ref[rows, :] = high
        low_ref[rows, :] = low
        out_ref[:, rows] = product_of(parts, high, low, NT)


def grad_kernel(recv_ref, labels_ref, high_ref, low_ref, logits_ref, probs_ref, out_ref):
    logits = sum_first(recv_ref)
    logits_ref[...] = logits
    expo = jnp.exp(logits)
    probs = expo / jnp.sum(expo, axis=0, keepdims=True)
    probs_ref[...] = probs
    onehot = (labels_ref[...] == lax.broadcasted_iota(jnp.int32, logits.shape, 0)).astype(F32)
    spread(out_ref, product_of(both_parts(probs - onehot), high_ref[...], low_ref[...], NN))


def resid_kernel(count, recv_ref, w_ref, high_ref, low_ref, resid_ref, out_ref):
    rows = high_ref.shape[0]
    resid = -(sum_first(recv_ref) / count + RIDGE * w_ref[...])
    resid_ref[...] = resid
    out_ref[:, rows:] = tile_of(total_of(resid * resid), 0.0)
    out_ref[:, :rows] = product_of(both_parts(resid), high_ref[...], low_ref[...], NT)


def product_kernel(count, recv_ref, resid_ref, high_ref, low_ref, product_ref, out_ref):
    rows = high_ref.shape[0]
    resid = resid_ref[...]
    product = sum_first(recv_ref) / count + RIDGE * resid
    product_ref[...] = product
    out_ref[:, rows:] = tile_of(total_of(resid * product), total_of(product * product))
    out_ref[:, :rows] = product_of(both_parts(product), high_ref[...], low_ref[...], NT)


def image_kernel(recv_ref, probs_ref, high_ref, low_ref, image_ref, tail_ref, out_ref):
    rows = high_ref.shape[0]
    image = sum_first(recv_ref, 0, rows)
    image_ref[...] = image
    tail_ref[...] = sum_first(recv_ref, rows, rows + LANES)
    terms = curved(probs_ref[...], image)
    spread(out_ref, product_of(both_parts(terms), high_ref[...], low_ref[...], NN))


def scalars(rr0, tail):
    along, square = tail[:1, :1], tail[:1, 1:2]
    alpha = rr0 / along
    rr1 = rr0 - 2.0 * alpha * along + alpha * alpha * square
    return alpha, rr1, rr1 / rr0


def second_kernel(recv_ref, tail_ref, probs_ref, image_ref, direction_ref, tail2_ref, out_ref):
    rows = image_ref.shape[1]
    tail = sum_first(recv_ref, rows, rows + LANES)
    tail2_ref[...] = tail
    alpha, rr1, beta = scalars(tail_ref[:1, :1], tail)
    image = image_ref[...]
    direction = image - alpha * sum_first(recv_ref, 0, rows) + beta * image
    direction_ref[...] = direction
    curvature = total_of(direction * curved(probs_ref[...], direction))
    out_ref[...] = jnp.broadcast_to(curvature, out_ref.shape)


def last_kernel(
    count, curvature_ref, tail_ref, tail2_ref, w_ref, resid_ref, product_ref, logits_ref,
    image_ref, direction_ref, weights_ref, scores_ref,
):
    rr0 = tail_ref[:1, :1]
    alpha, rr1, beta = scalars(rr0, tail2_ref[...])
    curvature = sum_first(curvature_ref)[:, :1]
    alpha1 = rr1 / (curvature / count + RIDGE * (rr1 + beta * beta * rr0))
    resid = resid_ref[...]
    direction = resid - alpha * product_ref[...] + beta * resid
    weights_ref[...] = w_ref[...] + (alpha * resid + alpha1 * direction)
    scores_ref[...] = logits_ref[...] + (alpha * image_ref[...] + alpha1 * direction_ref[...])


def call(kernel, shapes, *args, in_specs=None, scratch=(), limit=4):
    shapes = [jax.ShapeDtypeStruct(s, F32) if isinstance(s, tuple) else s for s in shapes]
    vmem = pl.BlockSpec(memory_space=pltpu.VMEM)
    return pl.pallas_call(
        kernel,
        out_shape=shapes,
        in_specs=in_specs or [vmem] * len(args),
        out_specs=[vmem] * len(shapes),
        scratch_shapes=list(scratch),
        compiler_params=pltpu.CompilerParams(vmem_limit_bytes=limit * 1024 * 1024),
    )(*args)


def exchange(blocks, axes):
    return lax.all_to_all(blocks, axes, 0, 0, tiled=True)


def relay(recv, axis):
    (blocks,) = call(relay_kernel, [(lax.axis_size(axis), *recv.shape[1:])], recv)
    return exchange(blocks, axis)


def over_feat(partial):
    return relay(lax.all_gather(partial, "core"), "y")


def over_cells(blocks):
    return relay(exchange(blocks, "z"), "x")


def on_device(features, labels, weights):
    rows, width = features.shape
    classes = weights.shape[0]
    count = rows * lax.axis_size(CELLS) * 1.0
    split = pltpu.VMEM((rows, width), BF16)
    cells, coeffs = (classes, rows), (classes, width)
    blocks = (lax.axis_size("z"), classes, width)
    padded, tile = (classes, rows + LANES), (classes, LANES)

    high, low, partial = call(
        first_kernel,
        [split, split, pltpu.VMEM(cells, F32)],
        weights,
        features,
        in_specs=[pl.BlockSpec(memory_space=pltpu.HBM)] * 2,
        limit=50,
        scratch=[
            pltpu.VMEM(coeffs, F32),
            pltpu.VMEM((rows, width), F32),
            pltpu.SemaphoreType.DMA((rows // CHUNK + 1,)),
        ],
    )
    logits, probs, partial = call(
        grad_kernel, [cells, cells, blocks], over_feat(partial), labels.reshape(1, rows), high, low
    )
    resid, partial = call(
        functools.partial(resid_kernel, count), [coeffs, padded], over_cells(partial), weights, high, low
    )
    image, tail, partial = call(
        image_kernel, [cells, tile, blocks], over_feat(partial), probs, high, low
    )
    product, partial = call(
        functools.partial(product_kernel, count), [coeffs, padded], over_cells(partial), resid, high, low
    )
    direction, tail2, curvature = call(
        second_kernel, [cells, tile, (lax.axis_size(CELLS), 1, LANES)], over_feat(partial), tail, probs, image
    )
    curvature = exchange(curvature, CELLS)
    return tuple(
        call(
            functools.partial(last_kernel, count),
            [coeffs, cells],
            curvature, tail, tail2, weights, resid, product, logits, image, direction,
        )
    )


def solution(mesh):
    grid = Mesh(mesh.devices.reshape(4, 16, 4, 2), CELLS + FEAT)
    return jax.shard_map(
        on_device,
        mesh=grid,
        in_specs=(P(CELLS, FEAT), P(CELLS), P(None, FEAT)),
        out_specs=(P(None, FEAT), P(None, CELLS)),
        check_vma=False,
    )
```

time: 171 us -> 141 us (0.82)
  blocking collectives: 94.5 us -> 130 us
  waiting for transfers between devices: 26 us -> 0 us
  matrix products: 18.4 us -> 0 us
  starting transfers between devices: 15.4 us -> 0 us
  Pallas kernels: 0 us -> 9.14 us
  other arithmetic: 6.1 us -> 0 us
  between operations: 6.18 us -> 0.69 us
  local copies, waits for them, and re-layouts: 3.98 us -> 0.01 us
    all_gather x0 -> x3, blocking collectives: none -> 27.9 us  [over_feat(): return relay(lax.all_gather(partial, 'core'), 'y')]
    all_to_all x3 -> x0, waiting for transfers between devices: 26 us -> none  [from_everyone(): lax.all_to_all(jnp.broadcast_to(array[None], (devices, *array.shape)), ax...]
    dot_general x5 -> x0, matrix products: 18.4 us -> none  [the longest x3 11.8 us: row_sums(): lax.dot_general(coeffs, features, (((1,), (1,)), ((), ())), precision=HIG...]
    all_to_all x3 -> x0, starting transfers between devices: 15.4 us -> none  [from_everyone(): lax.all_to_all(jnp.broadcast_to(array[None], (devices, *array.shape)), ax...]
    pallas_call x0 -> x12, Pallas kernels: none -> 9.14 us  [call(): pl.pallas_call(kernel, out_shape=shapes, in_specs=in_specs or [vmem] * le...]
    all_to_all x7 -> x8, blocking collectives: 94.5 us -> 103 us  [exchange(): return lax.all_to_all(blocks, axes, 0, 0, tiled=True)]
    reduce_sum x14 -> x0, other arithmetic: 2.84 us -> none  [the longest x1 0.71 us: on_device(): curvature = jnp.sum(direction_image * curved(direction_image))]
    select_n x3 -> x0, other arithmetic: 1.96 us -> none  [the longest x2 1.31 us: with_sums(): jnp.where(column == 0, first, jnp.where(column == 1, second, jnp.float32(...]
  transfers between devices with their start and end apart: 3 -> 0, of which waited for: 3 -> 0; matrix products, arithmetic and copies ran while one was open for 0% -> 0% of each run, Pallas kernels for 0% -> 0%
where the time goes in v2:
time: 141 us; the launch traced here: 140 us
  blocking collectives  130 us (92%)
  Pallas kernels  9.14 us (6%)
    all_to_all x8, blocking collectives, exchange(): return lax.all_to_all(blocks, axes, 0, 0, tiled=True)  103 us
    all_gather x3, blocking collectives, over_feat(): return relay(lax.all_gather(partial, 'core'), 'y')  27.9 us
    pallas_call x12, Pallas kernels, call(): pl.pallas_call(kernel, out_shape=shapes, in_specs=in_specs or [vmem] * le...  9.14 us

profile of v2, /device:TPU:1, one launch (start us, length us, event | category | flops | bytes accessed | tf_op | source)
XLA Modules:
  0.0 140.2 jit_solution(1593138478678502039)
XLA Ops:
  0.6 0.0 copy-start.1
  0.6 4.3 %shard_map.50 = (bf16[2048,512]{1,0:T(8,128)(2,1)S(1)}, bf16[2048,512]{1,0:T(8,128)(2,1)S(1)}, f32[8,2048]{1,0:T(8,128)S(1)}) custom-call(f32[8,512]{1,0:T(8,128)} %w_ref.5, f32[2048,512]{1,0:T(8,128)} %x_ref.1), custom_call_target="tpu_custom_call" | custom-call | tf_op jit(solution)/shard_map/pallas_call | solution.py:159
  5.0 8.4 %all-gather = f32[16,2048]{1,0:T(8,128)S(1)} all-gather(f32[8,2048]{1,0:T(8,128)S(1)} %get-tuple-element.18), channel_id=2, replica_groups=mesh['x'=4,'z'=16,'y'=4,'core'=2] {'core'}, dimensions={0}, use_global_device_ids=true | all-gather | bytes 196608 | tf_op jit(solution)/shard_map/all_gather | solution.py:179
  13.4 8.8 %all_to_all.40.recv_ref = f32[4,8,2048]{2,1,0:T(8,128)S(1)} all-to-all(f32[4,8,2048]{2,1,0:T(8,128)S(1)} %shard_map.51), channel_id=1, replica_groups=mesh['x'=4,'z'=16,'y'=4,'core'=2] {'y'}, dimensions={0} | all-to-all | bytes 524288 | tf_op jit(solution)/shard_map/all_to_all | solution.py:170
  22.2 0.0 copy-done.1
  22.2 0.0 copy-start
  22.2 0.7 shard_map.52
  22.9 23.1 %all_to_all.41.recv_ref = f32[16,8,512]{2,1,0:T(8,128)S(1)} all-to-all(f32[16,8,512]{2,1,0:T(8,128)S(1)} %get-tuple-element.21), channel_id=1, replica_groups=mesh['x'=4,'z'=16,'y'=4,'core'=2] {'z'}, dimensions={0} | all-to-all | bytes 524288 | tf_op jit(solution)/shard_map/all_to_all | solution.py:170
  46.0 8.3 %all_to_all.42.recv_ref = f32[4,8,512]{2,1,0:T(8,128)S(1)} all-to-all(f32[4,8,512]{2,1,0:T(8,128)S(1)} %shard_map.53), channel_id=1, replica_groups=mesh['x'=4,'z'=16,'y'=4,'core'=2] {'x'}, dimensions={0} | all-to-all | bytes 131072 | tf_op jit(solution)/shard_map/all_to_all | solution.py:170
  54.3 0.0 copy-done
  54.3 1.2 shard_map.54
  55.5 9.7 %all-gather.1 = f32[16,2176]{1,0:T(8,128)S(1)} all-gather(f32[8,2176]{1,0:T(8,128)S(1)} %get-tuple-element.22), channel_id=3, replica_groups=mesh['x'=4,'z'=16,'y'=4,'core'=2] {'core'}, dimensions={0}, use_global_device_ids=true | all-gather | bytes 208896 | tf_op jit(solution)/shard_map/all_gather | solution.py:179
  65.2 8.9 %all_to_all.43.recv_ref = f32[4,8,2176]{2,1,0:T(8,128)S(1)} all-to-all(f32[4,8,2176]{2,1,0:T(8,128)S(1)} %shard_map.55), channel_id=1, replica_groups=mesh['x'=4,'z'=16,'y'=4,'core'=2] {'y'}, dimensions={0} | all-to-all | bytes 557056 | tf_op jit(solution)/shard_map/all_to_all | solution.py:170
  74.2 0.7 shard_map.56
  74.8 17.9 %all_to_all.44.recv_ref = f32[16,8,512]{2,1,0:T(8,128)S(1)} all-to-all(f32[16,8,512]{2,1,0:T(8,128)S(1)} %get-tuple-element.24), channel_id=1, replica_groups=mesh['x'=4,'z'=16,'y'=4,'core'=2] {'z'}, dimensions={0} | all-to-all | bytes 524288 | tf_op jit(solution)/shard_map/all_to_all | solution.py:170
  92.8 6.8 %all_to_all.45.recv_ref = f32[4,8,512]{2,1,0:T(8,128)S(1)} all-to-all(f32[4,8,512]{2,1,0:T(8,128)S(1)} %shard_map.57), channel_id=1, replica_groups=mesh['x'=4,'z'=16,'y'=4,'core'=2] {'x'}, dimensions={0} | all-to-all | bytes 131072 | tf_op jit(solution)/shard_map/all_to_all | solution.py:170
  99.6 1.2 shard_map.58
  100.8 9.8 %all-gather.2 = f32[16,2176]{1,0:T(8,128)S(1)} all-gather(f32[8,2176]{1,0:T(8,128)S(1)} %get-tuple-element.26), channel_id=4, replica_groups=mesh['x'=4,'z'=16,'y'=4,'core'=2] {'core'}, dimensions={0}, use_global_device_ids=true | all-gather | bytes 208896 | tf_op jit(solution)/shard_map/all_gather | solution.py:179
  110.6 8.9 %all_to_all.46.recv_ref = f32[4,8,2176]{2,1,0:T(8,128)S(1)} all-to-all(f32[4,8,2176]{2,1,0:T(8,128)S(1)} %shard_map.59), channel_id=1, replica_groups=mesh['x'=4,'z'=16,'y'=4,'core'=2] {'y'}, dimensions={0} | all-to-all | bytes 557056 | tf_op jit(solution)/shard_map/all_to_all | solution.py:170
  119.6 0.2 shard_map.60
  119.8 19.7 %all_to_all.47.curvature_ref = f32[64,1,128]{2,1,0:T(1,128)S(1)} all-to-all(f32[64,1,128]{2,1,0:T(1,128)S(1)} %get-tuple-element.29), channel_id=1, replica_groups=mesh['x'=4,'z'=16,'y'=4,'core'=2] {'x','z'}, dimensions={0} | all-to-all | bytes 65536 | tf_op jit(solution)/shard_map/all_to_all | solution.py:170
  139.5 0.8 shard_map.61
  (5 shorter events, 0.1 us)
Async XLA Ops:
  0.6 21.5 %copy-start.1 = (s32[2048]{0:T(1024)S(1)}, s32[2048]{0:T(1024)}, u32[]{:S(2)}) copy-start(s32[2048]{0:T(1024)} %param.4) | copy-start | bytes 24580
  22.2 32.1 %copy-start = (f32[8,512]{1,0:T(8,128)S(1)}, f32[8,512]{1,0:T(8,128)}, u32[]{:S(2)}) copy-start(f32[8,512]{1,0:T(8,128)} %w_ref.5) | copy-start | bytes 49156

commit v3 on v2

--- a/solution.py
+++ b/solution.py
@@ -38,6 +38,10 @@
     return total
 
 
+def joined(ref):
+    return jnp.concatenate([ref[i] for i in range(ref.shape[0])], axis=1)
+
+
 def curved(probs, image):
     weighted = probs * image
     return weighted - probs * jnp.sum(weighted, axis=0, keepdims=True)
@@ -52,9 +56,15 @@
     return jnp.where(column == 0, first, jnp.where(column == 1, second, 0.0))
 
 
-def spread(ref, value, cols=slice(None)):
+def spread(ref, value):
     for i in range(ref.shape[0]):
-        ref[i, :, cols] = value
+        ref[i] = value
+
+
+def spread_blocks(ref, value):
+    step = value.shape[1] // ref.shape[0]
+    for i in range(ref.shape[0]):
+        ref[i] = value[:, i * step : (i + 1) * step]
 
 
 def relay_kernel(recv_ref, out_ref):
@@ -91,12 +101,12 @@
     probs = expo / jnp.sum(expo, axis=0, keepdims=True)
     probs_ref[...] = probs
     onehot = (labels_ref[...] == lax.broadcasted_iota(jnp.int32, logits.shape, 0)).astype(F32)
-    spread(out_ref, product_of(both_parts(probs - onehot), high_ref[...], low_ref[...], NN))
+    spread_blocks(out_ref, product_of(both_parts(probs - onehot), high_ref[...], low_ref[...], NN))
 
 
 def resid_kernel(count, recv_ref, w_ref, high_ref, low_ref, resid_ref, out_ref):
     rows = high_ref.shape[0]
-    resid = -(sum_first(recv_ref) / count + RIDGE * w_ref[...])
+    resid = -(joined(recv_ref) / count + RIDGE * w_ref[...])
     resid_ref[...] = resid
     out_ref[:, rows:] = tile_of(total_of(resid * resid), 0.0)
     out_ref[:, :rows] = product_of(both_parts(resid), high_ref[...], low_ref[...], NT)
@@ -105,7 +115,7 @@
 def product_kernel(count, recv_ref, resid_ref, high_ref, low_ref, product_ref, out_ref):
     rows = high_ref.shape[0]
     resid = resid_ref[...]
-    product = sum_first(recv_ref) / count + RIDGE * resid
+    product = joined(recv_ref) / count + RIDGE * resid
     product_ref[...] = product
     out_ref[:, rows:] = tile_of(total_of(resid * product), total_of(product * product))
     out_ref[:, :rows] = product_of(both_parts(product), high_ref[...], low_ref[...], NT)
@@ -117,7 +127,7 @@
     image_ref[...] = image
     tail_ref[...] = sum_first(recv_ref, rows, rows + LANES)
     terms = curved(probs_ref[...], image)
-    spread(out_ref, product_of(both_parts(terms), high_ref[...], low_ref[...], NN))
+    spread_blocks(out_ref, product_of(both_parts(terms), high_ref[...], low_ref[...], NN))
 
 
 def scalars(rr0, tail):
@@ -180,7 +190,7 @@
 
 
 def over_cells(blocks):
-    return relay(exchange(blocks, "z"), "x")
+    return relay(relay(exchange(blocks, "x"), "z"), "x")
 
 
 def on_device(features, labels, weights):
@@ -189,7 +199,8 @@
     count = rows * lax.axis_size(CELLS) * 1.0
     split = pltpu.VMEM((rows, width), BF16)
     cells, coeffs = (classes, rows), (classes, width)
-    blocks = (lax.axis_size("z"), classes, width)
+    planes = lax.axis_size("x")
+    blocks = (planes, classes, width // planes)
     padded, tile = (classes, rows + LANES), (classes, LANES)
 
     high, low, partial = call(

time: 141 us -> 141 us (level)
    all_gather x3, blocking collectives: 27.9 us -> 22.1 us  [over_feat(): return relay(lax.all_gather(partial, 'core'), 'y')]
    all_to_all x8 -> x10, blocking collectives: 103 us -> 108 us  [exchange(): return lax.all_to_all(blocks, axes, 0, 0, tiled=True)]
    pallas_call x12 -> x14, Pallas kernels: 9.14 us -> 9.09 us  [call(): pl.pallas_call(kernel, out_shape=shapes, in_specs=in_specs or [vmem] * le...]
where the time goes in v3:
time: 141 us; the launch traced here: 140 us
  blocking collectives  130 us (92%)
  Pallas kernels  9.09 us (6%)
    all_to_all x10, blocking collectives, exchange(): return lax.all_to_all(blocks, axes, 0, 0, tiled=True)  108 us
    all_gather x3, blocking collectives, over_feat(): return relay(lax.all_gather(partial, 'core'), 'y')  22.1 us
    pallas_call x14, Pallas kernels, call(): pl.pallas_call(kernel, out_shape=shapes, in_specs=in_specs or [vmem] * le...  9.09 us

profile of v3, /device:TPU:1, one launch (start us, length us, event | category | flops | bytes accessed | tf_op | source)
XLA Modules:
  0.0 139.9 jit_solution(15507305846846232368)
XLA Ops:
  0.6 0.0 copy-start.1
  0.6 4.3 %shard_map.50 = (bf16[2048,512]{1,0:T(8,128)(2,1)S(1)}, bf16[2048,512]{1,0:T(8,128)(2,1)S(1)}, f32[8,2048]{1,0:T(8,128)S(1)}) custom-call(f32[8,512]{1,0:T(8,128)} %w_ref.5, f32[2048,512]{1,0:T(8,128)} %x_ref.1), custom_call_target="tpu_custom_call" | custom-call | tf_op jit(solution)/shard_map/pallas_call | solution.py:169
  5.0 8.4 %all-gather = f32[16,2048]{1,0:T(8,128)S(1)} all-gather(f32[8,2048]{1,0:T(8,128)S(1)} %get-tuple-element.18), channel_id=2, replica_groups=mesh['x'=4,'z'=16,'y'=4,'core'=2] {'core'}, dimensions={0}, use_global_device_ids=true | all-gather | bytes 196608 | tf_op jit(solution)/shard_map/all_gather | solution.py:189
  13.4 8.8 %all_to_all.50.recv_ref = f32[4,8,2048]{2,1,0:T(8,128)S(1)} all-to-all(f32[4,8,2048]{2,1,0:T(8,128)S(1)} %shard_map.51), channel_id=1, replica_groups=mesh['x'=4,'z'=16,'y'=4,'core'=2] {'y'}, dimensions={0} | all-to-all | bytes 524288 | tf_op jit(solution)/shard_map/all_to_all | solution.py:180
  22.2 0.0 copy-done.1
  22.2 0.0 copy-start
  22.2 0.6 shard_map.52
  22.8 6.6 %all_to_all.51.recv_ref = f32[4,8,128]{2,1,0:T(8,128)S(1)} all-to-all(f32[4,8,128]{2,1,0:T(8,128)S(1)} %get-tuple-element.21), channel_id=1, replica_groups=mesh['x'=4,'z'=16,'y'=4,'core'=2] {'x'}, dimensions={0} | all-to-all | bytes 32768 | tf_op jit(solution)/shard_map/all_to_all | solution.py:180
  29.4 23.4 %all_to_all.52.recv_ref = f32[16,8,128]{2,1,0:T(8,128)S(1)} all-to-all(f32[16,8,128]{2,1,0:T(8,128)S(1)} %shard_map.53), channel_id=1, replica_groups=mesh['x'=4,'z'=16,'y'=4,'core'=2] {'z'}, dimensions={0} | all-to-all | bytes 131072 | tf_op jit(solution)/shard_map/all_to_all | solution.py:180
  52.8 6.6 %all_to_all.53.recv_ref = f32[4,8,128]{2,1,0:T(8,128)S(1)} all-to-all(f32[4,8,128]{2,1,0:T(8,128)S(1)} %shard_map.54), channel_id=1, replica_groups=mesh['x'=4,'z'=16,'y'=4,'core'=2] {'x'}, dimensions={0} | all-to-all | bytes 32768 | tf_op jit(solution)/shard_map/all_to_all | solution.py:180
  59.4 0.0 copy-done
  59.4 1.2 shard_map.55
  60.6 7.5 %all-gather.1 = f32[16,2176]{1,0:T(8,128)S(1)} all-gather(f32[8,2176]{1,0:T(8,128)S(1)} %get-tuple-element.22), channel_id=3, replica_groups=mesh['x'=4,'z'=16,'y'=4,'core'=2] {'core'}, dimensions={0}, use_global_device_ids=true | all-gather | bytes 208896 | tf_op jit(solution)/shard_map/all_gather | solution.py:189
  68.1 8.9 %all_to_all.54.recv_ref = f32[4,8,2176]{2,1,0:T(8,128)S(1)} all-to-all(f32[4,8,2176]{2,1,0:T(8,128)S(1)} %shard_map.56), channel_id=1, replica_groups=mesh['x'=4,'z'=16,'y'=4,'core'=2] {'y'}, dimensions={0} | all-to-all | bytes 557056 | tf_op jit(solution)/shard_map/all_to_all | solution.py:180
  77.1 0.6 shard_map.57
  77.7 6.6 %all_to_all.55.recv_ref = f32[4,8,128]{2,1,0:T(8,128)S(1)} all-to-all(f32[4,8,128]{2,1,0:T(8,128)S(1)} %get-tuple-element.24), channel_id=1, replica_groups=mesh['x'=4,'z'=16,'y'=4,'core'=2] {'x'}, dimensions={0} | all-to-all | bytes 32768 | tf_op jit(solution)/shard_map/all_to_all | solution.py:180
  84.3 14.3 %all_to_all.56.recv_ref = f32[16,8,128]{2,1,0:T(8,128)S(1)} all-to-all(f32[16,8,128]{2,1,0:T(8,128)S(1)} %shard_map.58), channel_id=1, replica_groups=mesh['x'=4,'z'=16,'y'=4,'core'=2] {'z'}, dimensions={0} | all-to-all | bytes 131072 | tf_op jit(solution)/shard_map/all_to_all | solution.py:180
  98.6 6.6 %all_to_all.57.recv_ref = f32[4,8,128]{2,1,0:T(8,128)S(1)} all-to-all(f32[4,8,128]{2,1,0:T(8,128)S(1)} %shard_map.59), channel_id=1, replica_groups=mesh['x'=4,'z'=16,'y'=4,'core'=2] {'x'}, dimensions={0} | all-to-all | bytes 32768 | tf_op jit(solution)/shard_map/all_to_all | solution.py:180
  105.2 1.2 shard_map.60
  106.4 6.2 %all-gather.2 = f32[16,2176]{1,0:T(8,128)S(1)} all-gather(f32[8,2176]{1,0:T(8,128)S(1)} %get-tuple-element.26), channel_id=4, replica_groups=mesh['x'=4,'z'=16,'y'=4,'core'=2] {'core'}, dimensions={0}, use_global_device_ids=true | all-gather | bytes 208896 | tf_op jit(solution)/shard_map/all_gather | solution.py:189
  112.6 8.9 %all_to_all.58.recv_ref = f32[4,8,2176]{2,1,0:T(8,128)S(1)} all-to-all(f32[4,8,2176]{2,1,0:T(8,128)S(1)} %shard_map.61), channel_id=1, replica_groups=mesh['x'=4,'z'=16,'y'=4,'core'=2] {'y'}, dimensions={0} | all-to-all | bytes 557056 | tf_op jit(solution)/shard_map/all_to_all | solution.py:180
  121.5 0.2 shard_map.62
  121.8 17.3 %all_to_all.59.curvature_ref = f32[64,1,128]{2,1,0:T(1,128)S(1)} all-to-all(f32[64,1,128]{2,1,0:T(1,128)S(1)} %get-tuple-element.29), channel_id=1, replica_groups=mesh['x'=4,'z'=16,'y'=4,'core'=2] {'x','z'}, dimensions={0} | all-to-all | bytes 65536 | tf_op jit(solution)/shard_map/all_to_all | solution.py:180
  139.1 0.8 shard_map.63
  (7 shorter events, 0.1 us)
Async XLA Ops:
  0.6 21.5 %copy-start.1 = (s32[2048]{0:T(1024)S(1)}, s32[2048]{0:T(1024)}, u32[]{:S(2)}) copy-start(s32[2048]{0:T(1024)} %param.4) | copy-start | bytes 24580
  22.2 37.2 %copy-start = (f32[8,512]{1,0:T(8,128)S(1)}, f32[8,512]{1,0:T(8,128)}, u32[]{:S(2)}) copy-start(f32[8,512]{1,0:T(8,128)} %w_ref.5) | copy-start | bytes 49156

commit v4 on v3

--- a/solution.py
+++ b/solution.py
@@ -2,6 +2,7 @@
 
 import jax
 import jax.numpy as jnp
+import numpy as np
 from jax import lax
 from jax.experimental import pallas as pl
 from jax.experimental.pallas import tpu as pltpu
@@ -9,9 +10,10 @@
 
 RIDGE = 0.01
 CELLS = ("x", "z")
+GRID = ("x", "z", "y", "core")
 FEAT = ("y", "core")
 LANES = 128
-CHUNK = 256
+CHUNK = 512
 F32 = jnp.float32
 BF16 = jnp.bfloat16
 NN = (((1,), (0,)), ((), ()))
@@ -71,8 +73,22 @@
     spread(out_ref, sum_first(recv_ref))
 
 
+def chip_rows(value, parts_of):
+    (high0, low0), (high1, low1) = parts_of
+    half = value.shape[1] // 2
+    left = product_of(both_parts(value[:, :half]), high0[...], low0[...], NT)
+    return left + product_of(both_parts(value[:, half:]), high1[...], low1[...], NT)
+
+
+def chip_columns(ref, value, parts_of):
+    parts = both_parts(value)
+    halves = [product_of(parts, high[...], low[...], NN) for high, low in parts_of]
+    spread_blocks(ref, jnp.concatenate(halves, axis=1))
+
+
 def first_kernel(w_ref, x_ref, high_ref, low_ref, out_ref, held_w, held, sems):
-    steps = held.shape[0] // CHUNK
+    total = held.shape[0]
+    steps = total // CHUNK
     copies = []
     weights = pltpu.make_async_copy(w_ref, held_w, sems.at[steps])
     weights.start()
@@ -83,6 +99,7 @@
         copies.append(copy)
     weights.wait()
     parts = both_parts(held_w[...])
+    out_ref[:, total:] = held_w[...]
     for i in range(steps):
         rows = pl.ds(i * CHUNK, CHUNK)
         copies[i].wait()
@@ -94,40 +111,58 @@
         out_ref[:, rows] = product_of(parts, high, low, NT)
 
 
-def grad_kernel(recv_ref, labels_ref, high_ref, low_ref, logits_ref, probs_ref, out_ref):
+def chip_kernel(recv_ref, weights_ref, out_ref):
+    rows = out_ref.shape[2]
+    weights_ref[...] = jnp.concatenate([recv_ref[0, :, rows:], recv_ref[1, :, rows:]], axis=1)
+    spread(out_ref, sum_first(recv_ref, 0, rows))
+
+
+def grad_kernel(
+    recv_ref, labels_ref, moved_ref, high1_ref, low1_ref,
+    logits_ref, probs_ref, out_ref, high0_ref, low0_ref,
+):
+    x = moved_ref[...]
+    high = x.astype(BF16)
+    high0_ref[...] = high
+    low0_ref[...] = (x - high.astype(F32)).astype(BF16)
     logits = sum_first(recv_ref)
     logits_ref[...] = logits
     expo = jnp.exp(logits)
     probs = expo / jnp.sum(expo, axis=0, keepdims=True)
     probs_ref[...] = probs
     onehot = (labels_ref[...] == lax.broadcasted_iota(jnp.int32, logits.shape, 0)).astype(F32)
-    spread_blocks(out_ref, product_of(both_parts(probs - onehot), high_ref[...], low_ref[...], NN))
-
-
-def resid_kernel(count, recv_ref, w_ref, high_ref, low_ref, resid_ref, out_ref):
-    rows = high_ref.shape[0]
+    chip_columns(out_ref, probs - onehot, ((high0_ref, low0_ref), (high1_ref, low1_ref)))
+
+
+def send_rows(out_ref, value, tile, parts_of):
+    rows = out_ref.shape[2] - LANES
+    image = chip_rows(value, parts_of)
+    for i in range(out_ref.shape[0]):
+        out_ref[i, :, :rows] = image
+        out_ref[i, :, rows:] = tile
+
+
+def resid_kernel(count, recv_ref, w_ref, high0, low0, high1, low1, resid_ref, out_ref):
     resid = -(joined(recv_ref) / count + RIDGE * w_ref[...])
     resid_ref[...] = resid
-    out_ref[:, rows:] = tile_of(total_of(resid * resid), 0.0)
-    out_ref[:, :rows] = product_of(both_parts(resid), high_ref[...], low_ref[...], NT)
-
-
-def product_kernel(count, recv_ref, resid_ref, high_ref, low_ref, product_ref, out_ref):
-    rows = high_ref.shape[0]
+    tile = tile_of(total_of(resid * resid), 0.0)
+    send_rows(out_ref, resid, tile, ((high0, low0), (high1, low1)))
+
+
+def product_kernel(count, recv_ref, resid_ref, high0, low0, high1, low1, product_ref, out_ref):
     resid = resid_ref[...]
     product = joined(recv_ref) / count + RIDGE * resid
     product_ref[...] = product
-    out_ref[:, rows:] = tile_of(total_of(resid * product), total_of(product * product))
-    out_ref[:, :rows] = product_of(both_parts(product), high_ref[...], low_ref[...], NT)
-
-
-def image_kernel(recv_ref, probs_ref, high_ref, low_ref, image_ref, tail_ref, out_ref):
-    rows = high_ref.shape[0]
+    tile = tile_of(total_of(resid * product), total_of(product * product))
+    send_rows(out_ref, product, tile, ((high0, low0), (high1, low1)))
+
+
+def image_kernel(recv_ref, probs_ref, high0, low0, high1, low1, image_ref, tail_ref, out_ref):
+    rows = image_ref.shape[1]
     image = sum_first(recv_ref, 0, rows)
     image_ref[...] = image
     tail_ref[...] = sum_first(recv_ref, rows, rows + LANES)
-    terms = curved(probs_ref[...], image)
-    spread_blocks(out_ref, product_of(both_parts(terms), high_ref[...], low_ref[...], NN))
+    chip_columns(out_ref, curved(probs_ref[...], image), ((high0, low0), (high1, low1)))
 
 
 def scalars(rr0, tail):
@@ -151,16 +186,24 @@
 
 def last_kernel(
     count, curvature_ref, tail_ref, tail2_ref, w_ref, resid_ref, product_ref, logits_ref,
-    image_ref, direction_ref, weights_ref, scores_ref,
+    image_ref, direction_ref, out_ref,
 ):
+    rows = logits_ref.shape[1]
     rr0 = tail_ref[:1, :1]
     alpha, rr1, beta = scalars(rr0, tail2_ref[...])
     curvature = sum_first(curvature_ref)[:, :1]
     alpha1 = rr1 / (curvature / count + RIDGE * (rr1 + beta * beta * rr0))
     resid = resid_ref[...]
     direction = resid - alpha * product_ref[...] + beta * resid
-    weights_ref[...] = w_ref[...] + (alpha * resid + alpha1 * direction)
-    scores_ref[...] = logits_ref[...] + (alpha * image_ref[...] + alpha1 * direction_ref[...])
+    out_ref[:, rows:] = w_ref[...] + (alpha * resid + alpha1 * direction)
+    out_ref[:, :rows] = logits_ref[...] + (alpha * image_ref[...] + alpha1 * direction_ref[...])
+
+
+def share_kernel(recv_ref, weights_ref, scores_ref):
+    rows, width = scores_ref.shape[1], weights_ref.shape[1]
+    scores_ref[...] = recv_ref[1, :, :rows]
+    start = pl.multiple_of(rows + width * lax.axis_index("core"), LANES)
+    weights_ref[...] = recv_ref[1, :, pl.ds(start, width)]
 
 
 def call(kernel, shapes, *args, in_specs=None, scratch=(), limit=4):
@@ -176,17 +219,29 @@
     )(*args)
 
 
-def exchange(blocks, axes):
-    return lax.all_to_all(blocks, axes, 0, 0, tiled=True)
+def groups(kind):
+    nx, nz, ny, nc = (lax.axis_size(axis) for axis in GRID)
+    place = np.arange(nx * nz * ny * nc).reshape(nx, nz, ny, nc)
+    near, work = place[..., 0], place[..., 1]
+    xyz = near.transpose(1, 0, 2)
+    if kind == "x":
+        pair = work.transpose(2, 1, 0).reshape(-1, nx), near.reshape(-1, ny)
+    elif kind == "y":
+        pair = work.reshape(-1, ny), near.transpose(1, 2, 0).reshape(-1, nx)
+    elif kind == "z":
+        pair = work.transpose(0, 2, 1).reshape(-1, nz), xyz.reshape(-1, nx * ny)
+    else:
+        pair = work.transpose(2, 0, 1).reshape(ny, -1), xyz.reshape(ny, -1)
+    return np.concatenate(pair).tolist()
+
+
+def exchange(blocks, kind):
+    return lax.all_to_all(blocks, GRID, 0, 0, axis_index_groups=groups(kind), tiled=True)
 
 
 def relay(recv, axis):
     (blocks,) = call(relay_kernel, [(lax.axis_size(axis), *recv.shape[1:])], recv)
     return exchange(blocks, axis)
-
-
-def over_feat(partial):
-    return relay(lax.all_gather(partial, "core"), "y")
 
 
 def over_cells(blocks):
@@ -198,51 +253,60 @@
     classes = weights.shape[0]
     count = rows * lax.axis_size(CELLS) * 1.0
     split = pltpu.VMEM((rows, width), BF16)
-    cells, coeffs = (classes, rows), (classes, width)
-    planes = lax.axis_size("x")
-    blocks = (planes, classes, width // planes)
-    padded, tile = (classes, rows + LANES), (classes, LANES)
-
-    high, low, partial = call(
+    planes, lines = lax.axis_size("x"), lax.axis_size("y")
+    cells, coeffs, tile = (classes, rows), (classes, 2 * width), (classes, LANES)
+    blocks = (planes, classes, 2 * width // planes)
+    padded = (lines, classes, rows + LANES)
+
+    moved = lax.ppermute(features, "core", [(0, 1)])
+    high1, low1, partial = call(
         first_kernel,
-        [split, split, pltpu.VMEM(cells, F32)],
+        [split, split, pltpu.VMEM((classes, rows + width), F32)],
         weights,
         features,
         in_specs=[pl.BlockSpec(memory_space=pltpu.HBM)] * 2,
-        limit=50,
+        limit=51,
         scratch=[
-            pltpu.VMEM(coeffs, F32),
+            pltpu.VMEM((classes, width), F32),
             pltpu.VMEM((rows, width), F32),
             pltpu.SemaphoreType.DMA((rows // CHUNK + 1,)),
         ],
     )
-    logits, probs, partial = call(
-        grad_kernel, [cells, cells, blocks], over_feat(partial), labels.reshape(1, rows), high, low
-    )
+    weights, partial = call(
+        chip_kernel, [coeffs, (lines, *cells)], lax.all_gather(partial, "core")
+    )
+    logits, probs, partial, high0, low0 = call(
+        grad_kernel,
+        [cells, cells, blocks, split, split],
+        exchange(partial, "y"), labels.reshape(1, rows), moved, high1, low1,
+    )
+    parts = (high0, low0, high1, low1)
     resid, partial = call(
-        functools.partial(resid_kernel, count), [coeffs, padded], over_cells(partial), weights, high, low
+        functools.partial(resid_kernel, count), [coeffs, padded], over_cells(partial), weights, *parts
     )
     image, tail, partial = call(
-        image_kernel, [cells, tile, blocks], over_feat(partial), probs, high, low
+        image_kernel, [cells, tile, blocks], exchange(partial, "y"), probs, *parts
     )
     product, partial = call(
-        functools.partial(product_kernel, count), [coeffs, padded], over_cells(partial), resid, high, low
+        functools.partial(product_kernel, count), [coeffs, padded], over_cells(partial), resid, *parts
     )
     direction, tail2, curvature = call(
-        second_kernel, [cells, tile, (lax.axis_size(CELLS), 1, LANES)], over_feat(partial), tail, probs, image
-    )
-    curvature = exchange(curvature, CELLS)
+        second_kernel,
+        [cells, tile, (lax.axis_size(CELLS), 1, LANES)],
+        exchange(partial, "y"), tail, probs, image,
+    )
+    (result,) = call(
+        functools.partial(last_kernel, count),
+        [(classes, rows + 2 * width)],
+        exchange(curvature, "cells"), tail, tail2, weights, resid, product, logits, image, direction,
+    )
     return tuple(
-        call(
-            functools.partial(last_kernel, count),
-            [coeffs, cells],
-            curvature, tail, tail2, weights, resid, product, logits, image, direction,
-        )
+        call(share_kernel, [(classes, width), cells], lax.all_gather(result, "core"))
     )
 
 
 def solution(mesh):
-    grid = Mesh(mesh.devices.reshape(4, 16, 4, 2), CELLS + FEAT)
+    grid = Mesh(mesh.devices.reshape(4, 16, 4, 2), GRID)
     return jax.shard_map(
         on_device,
         mesh=grid,

time: 141 us -> 137 us (0.972)
  blocking collectives: 130 us -> 123 us
  Pallas kernels: 9.09 us -> 11.4 us
    all_gather x3 -> x2, blocking collectives: 22.1 us -> 12.8 us  [the longest x1 10.9 us: on_device(): lax.all_gather(partial, 'core')]
    pallas_call x14 -> x13, Pallas kernels: 9.09 us -> 11.4 us  [call(): pl.pallas_call(kernel, out_shape=shapes, in_specs=in_specs or [vmem] * le...]
    all_to_all x10, blocking collectives: 108 us -> 110 us  [exchange(): lax.all_to_all(blocks, GRID, 0, 0, axis_index_groups=groups(kind), tiled=...]
  transfers between devices with their start and end apart: 0 -> 1, of which waited for: 0 -> 0; matrix products, arithmetic and copies ran while one was open for 0% -> 0% of each run, Pallas kernels for 0% -> 2%
where the time goes in v4:
time: 137 us; the launch traced here: 136 us
  blocking collectives  123 us (90%)
  Pallas kernels  11.4 us (8%)
    all_to_all x10, blocking collectives, exchange(): lax.all_to_all(blocks, GRID, 0, 0, axis_index_groups=groups(kind), tiled=...  110 us
    pallas_call x13, Pallas kernels, call(): pl.pallas_call(kernel, out_shape=shapes, in_specs=in_specs or [vmem] * le...  11.4 us
    all_gather x1, blocking collectives, on_device(): lax.all_gather(partial, 'core')  10.9 us
  transfers between devices with their start and end apart: 1, of which 0 were waited for; matrix products, arithmetic and copies ran while one was open for 0% of the time, Pallas kernels for 2%

profile of v4, /device:TPU:1, one launch (start us, length us, event | category | flops | bytes accessed | tf_op | source)
XLA Modules:
  0.0 136.0 jit_solution(16403941985626335924)
XLA Ops:
  0.6 0.0 copy-start
  0.6 1.3 collective-permute-start
  1.9 2.9 %shard_map.50 = (bf16[2048,512]{1,0:T(8,128)(2,1)S(1)}, bf16[2048,512]{1,0:T(8,128)(2,1)S(1)}, f32[8,2560]{1,0:T(8,128)S(1)}) custom-call(f32[8,512]{1,0:T(8,128)} %w_ref.1, f32[2048,512]{1,0:T(8,128)} %x_ref.1), custom_call_target="tpu_custom_call" | custom-call | tf_op jit(solution)/shard_map/pallas_call | solution.py:212
  4.8 10.9 %all-gather = f32[16,2560]{1,0:T(8,128)S(1)} all-gather(f32[8,2560]{1,0:T(8,128)S(1)} %get-tuple-element.22), channel_id=2, replica_groups=mesh['x'=4,'z'=16,'y'=4,'core'=2] {'core'}, dimensions={0}, use_global_device_ids=true | all-gather | bytes 245760 | tf_op jit(solution)/shard_map/all_gather | solution.py:276
  15.8 8.1 %all_to_all.50.recv_ref = f32[4,8,2048]{2,1,0:T(8,128)S(1)} all-to-all(f32[4,8,2048]{2,1,0:T(8,128)S(1)} %get-tuple-element.23), channel_id=1, replica_groups={{1,3,5,7},{9,11,13,15},{17,19,21,23},{25,27,29,31},{33,35,37,39},{41,43..., dimensions={0} | all-to-all | bytes 524288 | tf_op jit(solution)/shard_map/all_to_all | solution.py:239
  23.9 0.0 collective-permute-done.moved_ref
  23.9 0.0 copy-done
  23.9 1.7 %shard_map.52 = (f32[8,2048]{1,0:T(8,128)S(1)}, f32[8,2048]{1,0:T(8,128)S(1)}, f32[4,8,256]{2,1,0:T(8,128)S(1)}, bf16[2048,512]{1,0:T(8,128)(2,1)S(1)}, bf16[2048,512]{1,0:T(8,128)(2,1)S(1)}) custom-call(f32[4,8,2048]{2,1,0:T(8,128)S(1)} %all_to_all.50.recv_ref, s32[1,2048]{1,0:T(1,128)S(1)} %bitcast.5, f32[2048,512]{1,0:T(8,128)S(1)} %collective-permute-done.moved_ref, ...), custom_call_target="tpu_custom_call" | custom-call | tf_op jit(solution)/shard_map/pallas_call | solution.py:212
  25.5 6.7 %all_to_all.51.recv_ref = f32[4,8,256]{2,1,0:T(8,128)S(1)} all-to-all(f32[4,8,256]{2,1,0:T(8,128)S(1)} %get-tuple-element.26), channel_id=1, replica_groups={{1,129,257,385},{9,137,265,393},{17,145,273,401},{25,153,281,409},{33,1..., dimensions={0} | all-to-all | bytes 65536 | tf_op jit(solution)/shard_map/all_to_all | solution.py:239
  32.2 24.6 %all_to_all.52.recv_ref = f32[16,8,256]{2,1,0:T(8,128)S(1)} all-to-all(f32[16,8,256]{2,1,0:T(8,128)S(1)} %shard_map.53), channel_id=1, replica_groups={{1,9,17,25,33,41,49,57,65,73,81,89,97,105,113,121},{3,11,19,27,35,43,51..., dimensions={0} | all-to-all | bytes 262144 | tf_op jit(solution)/shard_map/all_to_all | solution.py:239
  56.9 6.8 %all_to_all.53.recv_ref = f32[4,8,256]{2,1,0:T(8,128)S(1)} all-to-all(f32[4,8,256]{2,1,0:T(8,128)S(1)} %shard_map.54), channel_id=1, replica_groups={{1,129,257,385},{9,137,265,393},{17,145,273,401},{25,153,281,409},{33,1..., dimensions={0} | all-to-all | bytes 65536 | tf_op jit(solution)/shard_map/all_to_all | solution.py:239
  63.7 2.3 %shard_map.55 = (f32[8,1024]{1,0:T(8,128)S(1)}, f32[4,8,2176]{2,1,0:T(8,128)S(1)}) custom-call(f32[4,8,256]{2,1,0:T(8,128)S(1)} %all_to_all.53.recv_ref, f32[8,1024]{1,0:T(8,128)S(1)} %get-tuple-element.27.w_ref, bf16[2048,512]{1,0:T(8,128)(2,1)S(1)} %get-tuple-element.28.high0, bf16[2048,512]{1,0:T(8,128)(2,1)S(1)} %get-tuple-element.29.low0, ...), custom_call_target="tpu_custom_call" | custom-call | tf_op jit(solution)/shard_map/pallas_call | solution.py:212
  66.0 8.2 %all_to_all.54.recv_ref = f32[4,8,2176]{2,1,0:T(8,128)S(1)} all-to-all(f32[4,8,2176]{2,1,0:T(8,128)S(1)} %get-tuple-element.30), channel_id=1, replica_groups={{1,3,5,7},{9,11,13,15},{17,19,21,23},{25,27,29,31},{33,35,37,39},{41,43..., dimensions={0} | all-to-all | bytes 557056 | tf_op jit(solution)/shard_map/all_to_all | solution.py:239
  74.1 1.2 shard_map.56
  75.3 6.8 %all_to_all.55.recv_ref = f32[4,8,256]{2,1,0:T(8,128)S(1)} all-to-all(f32[4,8,256]{2,1,0:T(8,128)S(1)} %get-tuple-element.32), channel_id=1, replica_groups={{1,129,257,385},{9,137,265,393},{17,145,273,401},{25,153,281,409},{33,1..., dimensions={0} | all-to-all | bytes 65536 | tf_op jit(solution)/shard_map/all_to_all | solution.py:239
  82.2 15.3 %all_to_all.56.recv_ref = f32[16,8,256]{2,1,0:T(8,128)S(1)} all-to-all(f32[16,8,256]{2,1,0:T(8,128)S(1)} %shard_map.57), channel_id=1, replica_groups={{1,9,17,25,33,41,49,57,65,73,81,89,97,105,113,121},{3,11,19,27,35,43,51..., dimensions={0} | all-to-all | bytes 262144 | tf_op jit(solution)/shard_map/all_to_all | solution.py:239
  97.5 6.7 %all_to_all.57.recv_ref = f32[4,8,256]{2,1,0:T(8,128)S(1)} all-to-all(f32[4,8,256]{2,1,0:T(8,128)S(1)} %shard_map.58), channel_id=1, replica_groups={{1,129,257,385},{9,137,265,393},{17,145,273,401},{25,153,281,409},{33,1..., dimensions={0} | all-to-all | bytes 65536 | tf_op jit(solution)/shard_map/all_to_all | solution.py:239
  104.1 2.3 %shard_map.59 = (f32[8,1024]{1,0:T(8,128)S(1)}, f32[4,8,2176]{2,1,0:T(8,128)S(1)}) custom-call(f32[4,8,256]{2,1,0:T(8,128)S(1)} %all_to_all.57.recv_ref, f32[8,1024]{1,0:T(8,128)S(1)} %get-tuple-element.33.resid_ref, bf16[2048,512]{1,0:T(8,128)(2,1)S(1)} %get-tuple-element.28.high0, bf16[2048,512]{1,0:T(8,128)(2,1)S(1)} %get-tuple-element.29.low0, ...), custom_call_target="tpu_custom_call" | custom-call | tf_op jit(solution)/shard_map/pallas_call | solution.py:212
  106.4 8.0 %all_to_all.58.recv_ref = f32[4,8,2176]{2,1,0:T(8,128)S(1)} all-to-all(f32[4,8,2176]{2,1,0:T(8,128)S(1)} %get-tuple-element.34), channel_id=1, replica_groups={{1,3,5,7},{9,11,13,15},{17,19,21,23},{25,27,29,31},{33,35,37,39},{41,43..., dimensions={0} | all-to-all | bytes 557056 | tf_op jit(solution)/shard_map/all_to_all | solution.py:239
  114.4 0.2 shard_map.60
  114.6 18.6 %all_to_all.59.curvature_ref = f32[64,1,128]{2,1,0:T(1,128)S(1)} all-to-all(f32[64,1,128]{2,1,0:T(1,128)S(1)} %get-tuple-element.37), channel_id=1, replica_groups={{1,9,17,25,33,41,49,57,65,73,81,89,97,105,113,121,129,137,145,153,161,1..., dimensions={0} | all-to-all | bytes 65536 | tf_op jit(solution)/shard_map/all_to_all | solution.py:239
  133.2 0.1 shard_map.61
  133.4 1.9 %all-gather.1 = f32[16,3072]{1,0:T(8,128)S(1)} all-gather(f32[8,3072]{1,0:T(8,128)S(1)} %shard_map.61), channel_id=3, replica_groups=mesh['x'=4,'z'=16,'y'=4,'core'=2] {'core'}, dimensions={0}, use_global_device_ids=true | all-gather | bytes 294912 | tf_op jit(solution)/shard_map/all_gather | solution.py:304
  135.3 0.6 shard_map.62
  (5 shorter events, 0.1 us)
Async XLA Ops:
  0.6 23.2 %copy-start = (s32[2048]{0:T(1024)S(1)}, s32[2048]{0:T(1024)}, u32[]{:S(2)}) copy-start(s32[2048]{0:T(1024)} %param.4) | copy-start | bytes 24580
  0.6 23.2 %collective-permute-start = (f32[2048,512]{1,0:T(8,128)}, f32[2048,512]{1,0:T(8,128)S(1)}, u32[]{:S(2)}, u32[]{:S(2)}) collective-permute-start(f32[2048,512]{1,0:T(8,128)} %x_ref.1), channel_id=1, source_target_pairs={{0,1},{2,3},{4,5},{6,7},{8,9},{10,11},{12,13},{14,15},{16,17},{18,... | collective-permute-start | bytes 12582920 | tf_op jit(solution)/shard_map/ppermute | solution.py:261

commit v5 on v4

--- a/solution.py
+++ b/solution.py
@@ -86,7 +86,7 @@
     spread_blocks(ref, jnp.concatenate(halves, axis=1))
 
 
-def first_kernel(w_ref, x_ref, high_ref, low_ref, out_ref, held_w, held, sems):
+def first_kernel(w_ref, x_ref, high_ref, low_ref, out_ref, held, held_w, sems):
     total = held.shape[0]
     steps = total // CHUNK
     copies = []
@@ -258,23 +258,26 @@
     blocks = (planes, classes, 2 * width // planes)
     padded = (lines, classes, rows + LANES)
 
-    moved = lax.ppermute(features, "core", [(0, 1)])
-    high1, low1, partial = call(
+    high1, low1, partial, held = call(
         first_kernel,
-        [split, split, pltpu.VMEM((classes, rows + width), F32)],
+        [
+            split,
+            split,
+            pltpu.VMEM((classes, rows + width), F32),
+            pltpu.VMEM((rows, width), F32),
+        ],
         weights,
         features,
         in_specs=[pl.BlockSpec(memory_space=pltpu.HBM)] * 2,
-        limit=51,
+        limit=49,
         scratch=[
             pltpu.VMEM((classes, width), F32),
-            pltpu.VMEM((rows, width), F32),
             pltpu.SemaphoreType.DMA((rows // CHUNK + 1,)),
         ],
     )
-    weights, partial = call(
-        chip_kernel, [coeffs, (lines, *cells)], lax.all_gather(partial, "core")
-    )
+    gathered, held = lax.optimization_barrier((lax.all_gather(partial, "core"), held))
+    moved = lax.ppermute(held, "core", [(0, 1)])
+    weights, partial = call(chip_kernel, [coeffs, (lines, *cells)], gathered)
     logits, probs, partial, high0, low0 = call(
         grad_kernel,
         [cells, cells, blocks, split, split],

time: 137 us -> 134 us (0.978)
  blocking collectives: 123 us -> 120 us
    all_gather x1, blocking collectives: 10.9 us -> 8.4 us  [on_device(): lax.all_gather(partial, 'core')]
  transfers between devices with their start and end apart: 1 -> 1, of which waited for: 0 -> 0; matrix products, arithmetic and copies ran while one was open for 0% -> 0% of each run, Pallas kernels for 2% -> 0%
where the time goes in v5:
time: 134 us; the launch traced here: 133 us
  blocking collectives  120 us (90%)
  Pallas kernels  11.5 us (9%)
    all_to_all x10, blocking collectives, exchange(): lax.all_to_all(blocks, GRID, 0, 0, axis_index_groups=groups(kind), tiled=...  109 us
    pallas_call x13, Pallas kernels, call(): pl.pallas_call(kernel, out_shape=shapes, in_specs=in_specs or [vmem] * le...  11.5 us
    all_gather x1, blocking collectives, on_device(): lax.all_gather(partial, 'core')  8.4 us
  transfers between devices with their start and end apart: 1, of which 0 were waited for; matrix products, arithmetic and copies ran while one was open for 0% of the time, Pallas kernels for 0%

profile of v5, /device:TPU:1, one launch (start us, length us, event | category | flops | bytes accessed | tf_op | source)
XLA Modules:
  0.0 133.1 jit_solution(12303253908876992254)
XLA Ops:
  0.6 0.0 copy-start
  0.6 2.9 %shard_map.50 = (bf16[2048,512]{1,0:T(8,128)(2,1)S(1)}, bf16[2048,512]{1,0:T(8,128)(2,1)S(1)}, f32[8,2560]{1,0:T(8,128)S(1)}, f32[2048,512]{1,0:T(8,128)S(1)}) custom-call(f32[8,512]{1,0:T(8,128)} %w_ref.1, f32[2048,512]{1,0:T(8,128)} %x_ref.1), custom_call_target="tpu_custom_call" | custom-call | tf_op jit(solution)/shard_map/pallas_call | solution.py:212
  3.6 8.4 %all-gather = f32[16,2560]{1,0:T(8,128)S(1)} all-gather(f32[8,2560]{1,0:T(8,128)S(1)} %get-tuple-element.25), channel_id=2, replica_groups=mesh['x'=4,'z'=16,'y'=4,'core'=2] {'core'}, dimensions={0}, use_global_device_ids=true | all-gather | bytes 245760 | tf_op jit(solution)/shard_map/all_gather | solution.py:278
  12.0 1.3 collective-permute-start
  13.3 7.9 %all_to_all.50.recv_ref = f32[4,8,2048]{2,1,0:T(8,128)S(1)} all-to-all(f32[4,8,2048]{2,1,0:T(8,128)S(1)} %get-tuple-element.28), channel_id=1, replica_groups={{1,3,5,7},{9,11,13,15},{17,19,21,23},{25,27,29,31},{33,35,37,39},{41,43..., dimensions={0} | all-to-all | bytes 524288 | tf_op jit(solution)/shard_map/all_to_all | solution.py:239
  21.2 0.0 collective-permute-done.moved_ref
  21.2 0.0 copy-done
  21.2 1.7 %shard_map.52 = (f32[8,2048]{1,0:T(8,128)S(1)}, f32[8,2048]{1,0:T(8,128)S(1)}, f32[4,8,256]{2,1,0:T(8,128)S(1)}, bf16[2048,512]{1,0:T(8,128)(2,1)S(1)}, bf16[2048,512]{1,0:T(8,128)(2,1)S(1)}) custom-call(f32[4,8,2048]{2,1,0:T(8,128)S(1)} %all_to_all.50.recv_ref, s32[1,2048]{1,0:T(1,128)S(1)} %bitcast.5, f32[2048,512]{1,0:T(8,128)S(1)} %collective-permute-done.moved_ref, ...), custom_call_target="tpu_custom_call" | custom-call | tf_op jit(solution)/shard_map/pallas_call | solution.py:212
  22.9 6.7 %all_to_all.51.recv_ref = f32[4,8,256]{2,1,0:T(8,128)S(1)} all-to-all(f32[4,8,256]{2,1,0:T(8,128)S(1)} %get-tuple-element.32), channel_id=1, replica_groups={{1,129,257,385},{9,137,265,393},{17,145,273,401},{25,153,281,409},{33,1..., dimensions={0} | all-to-all | bytes 65536 | tf_op jit(solution)/shard_map/all_to_all | solution.py:239
  29.6 24.4 %all_to_all.52.recv_ref = f32[16,8,256]{2,1,0:T(8,128)S(1)} all-to-all(f32[16,8,256]{2,1,0:T(8,128)S(1)} %shard_map.53), channel_id=1, replica_groups={{1,9,17,25,33,41,49,57,65,73,81,89,97,105,113,121},{3,11,19,27,35,43,51..., dimensions={0} | all-to-all | bytes 262144 | tf_op jit(solution)/shard_map/all_to_all | solution.py:239
  54.0 6.7 %all_to_all.53.recv_ref = f32[4,8,256]{2,1,0:T(8,128)S(1)} all-to-all(f32[4,8,256]{2,1,0:T(8,128)S(1)} %shard_map.54), channel_id=1, replica_groups={{1,129,257,385},{9,137,265,393},{17,145,273,401},{25,153,281,409},{33,1..., dimensions={0} | all-to-all | bytes 65536 | tf_op jit(solution)/shard_map/all_to_all | solution.py:239
  60.7 2.3 %shard_map.55 = (f32[8,1024]{1,0:T(8,128)S(1)}, f32[4,8,2176]{2,1,0:T(8,128)S(1)}) custom-call(f32[4,8,256]{2,1,0:T(8,128)S(1)} %all_to_all.53.recv_ref, f32[8,1024]{1,0:T(8,128)S(1)} %get-tuple-element.33.w_ref, bf16[2048,512]{1,0:T(8,128)(2,1)S(1)} %get-tuple-element.34.high0, bf16[2048,512]{1,0:T(8,128)(2,1)S(1)} %get-tuple-element.35.low0, ...), custom_call_target="tpu_custom_call" | custom-call | tf_op jit(solution)/shard_map/pallas_call | solution.py:212
  62.9 8.0 %all_to_all.54.recv_ref = f32[4,8,2176]{2,1,0:T(8,128)S(1)} all-to-all(f32[4,8,2176]{2,1,0:T(8,128)S(1)} %get-tuple-element.36), channel_id=1, replica_groups={{1,3,5,7},{9,11,13,15},{17,19,21,23},{25,27,29,31},{33,35,37,39},{41,43..., dimensions={0} | all-to-all | bytes 557056 | tf_op jit(solution)/shard_map/all_to_all | solution.py:239
  70.9 1.2 shard_map.56
  72.1 6.7 %all_to_all.55.recv_ref = f32[4,8,256]{2,1,0:T(8,128)S(1)} all-to-all(f32[4,8,256]{2,1,0:T(8,128)S(1)} %get-tuple-element.38), channel_id=1, replica_groups={{1,129,257,385},{9,137,265,393},{17,145,273,401},{25,153,281,409},{33,1..., dimensions={0} | all-to-all | bytes 65536 | tf_op jit(solution)/shard_map/all_to_all | solution.py:239
  78.8 15.8 %all_to_all.56.recv_ref = f32[16,8,256]{2,1,0:T(8,128)S(1)} all-to-all(f32[16,8,256]{2,1,0:T(8,128)S(1)} %shard_map.57), channel_id=1, replica_groups={{1,9,17,25,33,41,49,57,65,73,81,89,97,105,113,121},{3,11,19,27,35,43,51..., dimensions={0} | all-to-all | bytes 262144 | tf_op jit(solution)/shard_map/all_to_all | solution.py:239
  94.6 7.1 %all_to_all.57.recv_ref = f32[4,8,256]{2,1,0:T(8,128)S(1)} all-to-all(f32[4,8,256]{2,1,0:T(8,128)S(1)} %shard_map.58), channel_id=1, replica_groups={{1,129,257,385},{9,137,265,393},{17,145,273,401},{25,153,281,409},{33,1..., dimensions={0} | all-to-all | bytes 65536 | tf_op jit(solution)/shard_map/all_to_all | solution.py:239
  101.7 2.3 %shard_map.59 = (f32[8,1024]{1,0:T(8,128)S(1)}, f32[4,8,2176]{2,1,0:T(8,128)S(1)}) custom-call(f32[4,8,256]{2,1,0:T(8,128)S(1)} %all_to_all.57.recv_ref, f32[8,1024]{1,0:T(8,128)S(1)} %get-tuple-element.39.resid_ref, bf16[2048,512]{1,0:T(8,128)(2,1)S(1)} %get-tuple-element.34.high0, bf16[2048,512]{1,0:T(8,128)(2,1)S(1)} %get-tuple-element.35.low0, ...), custom_call_target="tpu_custom_call" | custom-call | tf_op jit(solution)/shard_map/pallas_call | solution.py:212
  104.0 8.0 %all_to_all.58.recv_ref = f32[4,8,2176]{2,1,0:T(8,128)S(1)} all-to-all(f32[4,8,2176]{2,1,0:T(8,128)S(1)} %get-tuple-element.40), channel_id=1, replica_groups={{1,3,5,7},{9,11,13,15},{17,19,21,23},{25,27,29,31},{33,35,37,39},{41,43..., dimensions={0} | all-to-all | bytes 557056 | tf_op jit(solution)/shard_map/all_to_all | solution.py:239
  111.9 0.2 shard_map.60
  112.2 18.2 %all_to_all.59.curvature_ref = f32[64,1,128]{2,1,0:T(1,128)S(1)} all-to-all(f32[64,1,128]{2,1,0:T(1,128)S(1)} %get-tuple-element.43), channel_id=1, replica_groups={{1,9,17,25,33,41,49,57,65,73,81,89,97,105,113,121,129,137,145,153,161,1..., dimensions={0} | all-to-all | bytes 65536 | tf_op jit(solution)/shard_map/all_to_all | solution.py:239
  130.4 0.1 shard_map.61
  130.5 1.9 %all-gather.1 = f32[16,3072]{1,0:T(8,128)S(1)} all-gather(f32[8,3072]{1,0:T(8,128)S(1)} %shard_map.61), channel_id=3, replica_groups=mesh['x'=4,'z'=16,'y'=4,'core'=2] {'core'}, dimensions={0}, use_global_device_ids=true | all-gather | bytes 294912 | tf_op jit(solution)/shard_map/all_gather | solution.py:307
  132.5 0.6 shard_map.62
  (5 shorter events, 0.1 us)
Async XLA Ops:
  0.6 20.6 %copy-start = (s32[2048]{0:T(1024)S(1)}, s32[2048]{0:T(1024)}, u32[]{:S(2)}) copy-start(s32[2048]{0:T(1024)} %param.4) | copy-start | bytes 24580
  12.0 9.2 %collective-permute-start = (f32[2048,512]{1,0:T(8,128)S(1)}, f32[2048,512]{1,0:T(8,128)S(1)}, u32[]{:S(2)}, u32[]{:S(2)}) collective-permute-start(f32[2048,512]{1,0:T(8,128)S(1)} %get-tuple-element.29), channel_id=1, source_target_pairs={{0,1},{2,3},{4,5},{6,7},{8,9},{10,11},{12,13},{14,15},{16,17},{18,... | collective-permute-start | bytes 12582920 | tf_op jit(solution)/shard_map/ppermute | solution.py:279

commit v6 on v5

--- a/solution.py
+++ b/solution.py
@@ -40,8 +40,12 @@
     return total
 
 
-def joined(ref):
-    return jnp.concatenate([ref[i] for i in range(ref.shape[0])], axis=1)
+def joined(ref, width):
+    pieces = width // ref.shape[2]
+    line = ref.shape[0] // pieces
+    return jnp.concatenate(
+        [sum_first(ref.at[pl.ds(i * line, line)]) for i in range(pieces)], axis=1
+    )
 
 
 def curved(probs, image):
@@ -143,7 +147,7 @@
 
 
 def resid_kernel(count, recv_ref, w_ref, high0, low0, high1, low1, resid_ref, out_ref):
-    resid = -(joined(recv_ref) / count + RIDGE * w_ref[...])
+    resid = -(joined(recv_ref, w_ref.shape[1]) / count + RIDGE * w_ref[...])
     resid_ref[...] = resid
     tile = tile_of(total_of(resid * resid), 0.0)
     send_rows(out_ref, resid, tile, ((high0, low0), (high1, low1)))
@@ -151,7 +155,7 @@
 
 def product_kernel(count, recv_ref, resid_ref, high0, low0, high1, low1, product_ref, out_ref):
     resid = resid_ref[...]
-    product = joined(recv_ref) / count + RIDGE * resid
+    product = joined(recv_ref, resid.shape[1]) / count + RIDGE * resid
     product_ref[...] = product
     tile = tile_of(total_of(resid * product), total_of(product * product))
     send_rows(out_ref, product, tile, ((high0, low0), (high1, low1)))
@@ -239,13 +243,10 @@
     return lax.all_to_all(blocks, GRID, 0, 0, axis_index_groups=groups(kind), tiled=True)
 
 
-def relay(recv, axis):
-    (blocks,) = call(relay_kernel, [(lax.axis_size(axis), *recv.shape[1:])], recv)
-    return exchange(blocks, axis)
-
-
 def over_cells(blocks):
-    return relay(relay(exchange(blocks, "x"), "z"), "x")
+    recv = exchange(blocks, "x")
+    (blocks,) = call(relay_kernel, [(lax.axis_size(CELLS), *recv.shape[1:])], recv)
+    return exchange(blocks, "cells")
 
 
 def on_device(features, labels, weights):

time: 134 us -> 153 us (1.14)
  blocking collectives: 120 us -> 139 us
    all_to_all x10 -> x8, blocking collectives: 109 us -> 129 us  [exchange(): lax.all_to_all(blocks, GRID, 0, 0, axis_index_groups=groups(kind), tiled=...]
    pallas_call x13 -> x11, Pallas kernels: 11.5 us -> 11.4 us  [call(): pl.pallas_call(kernel, out_shape=shapes, in_specs=in_specs or [vmem] * le...]
where the time goes in v6:
time: 153 us; the launch traced here: 152 us
  blocking collectives  139 us (91%)
  Pallas kernels  11.4 us (7%)
    all_to_all x8, blocking collectives, exchange(): lax.all_to_all(blocks, GRID, 0, 0, axis_index_groups=groups(kind), tiled=...  129 us
    pallas_call x11, Pallas kernels, call(): pl.pallas_call(kernel, out_shape=shapes, in_specs=in_specs or [vmem] * le...  11.4 us
    all_gather x1, blocking collectives, on_device(): lax.all_gather(partial, 'core')  8.4 us
  transfers between devices with their start and end apart: 1, of which 0 were waited for; matrix products, arithmetic and copies ran while one was open for 0% of the time, Pallas kernels for 0%

profile of v6, /device:TPU:1, one launch (start us, length us, event | category | flops | bytes accessed | tf_op | source)
XLA Modules:
  0.0 152.5 jit_solution(4119860809404385928)
XLA Ops:
  0.6 0.0 copy-start
  0.6 2.9 %shard_map.50 = (bf16[2048,512]{1,0:T(8,128)(2,1)S(1)}, bf16[2048,512]{1,0:T(8,128)(2,1)S(1)}, f32[8,2560]{1,0:T(8,128)S(1)}, f32[2048,512]{1,0:T(8,128)S(1)}) custom-call(f32[8,512]{1,0:T(8,128)} %w_ref.1, f32[2048,512]{1,0:T(8,128)} %x_ref.1), custom_call_target="tpu_custom_call" | custom-call | tf_op jit(solution)/shard_map/pallas_call | solution.py:216
  3.6 8.4 %all-gather = f32[16,2560]{1,0:T(8,128)S(1)} all-gather(f32[8,2560]{1,0:T(8,128)S(1)} %get-tuple-element.25), channel_id=2, replica_groups=mesh['x'=4,'z'=16,'y'=4,'core'=2] {'core'}, dimensions={0}, use_global_device_ids=true | all-gather | bytes 245760 | tf_op jit(solution)/shard_map/all_gather | solution.py:279
  12.0 1.3 collective-permute-start
  13.3 7.9 %all_to_all.40.recv_ref = f32[4,8,2048]{2,1,0:T(8,128)S(1)} all-to-all(f32[4,8,2048]{2,1,0:T(8,128)S(1)} %get-tuple-element.28), channel_id=1, replica_groups={{1,3,5,7},{9,11,13,15},{17,19,21,23},{25,27,29,31},{33,35,37,39},{41,43..., dimensions={0} | all-to-all | bytes 524288 | tf_op jit(solution)/shard_map/all_to_all | solution.py:243
  21.2 0.0 collective-permute-done.moved_ref
  21.2 0.0 copy-done
  21.2 1.7 %shard_map.52 = (f32[8,2048]{1,0:T(8,128)S(1)}, f32[8,2048]{1,0:T(8,128)S(1)}, f32[4,8,256]{2,1,0:T(8,128)S(1)}, bf16[2048,512]{1,0:T(8,128)(2,1)S(1)}, bf16[2048,512]{1,0:T(8,128)(2,1)S(1)}) custom-call(f32[4,8,2048]{2,1,0:T(8,128)S(1)} %all_to_all.40.recv_ref, s32[1,2048]{1,0:T(1,128)S(1)} %bitcast.5, f32[2048,512]{1,0:T(8,128)S(1)} %collective-permute-done.moved_ref, ...), custom_call_target="tpu_custom_call" | custom-call | tf_op jit(solution)/shard_map/pallas_call | solution.py:216
  22.9 6.7 %all_to_all.41.recv_ref = f32[4,8,256]{2,1,0:T(8,128)S(1)} all-to-all(f32[4,8,256]{2,1,0:T(8,128)S(1)} %get-tuple-element.32), channel_id=1, replica_groups={{1,129,257,385},{9,137,265,393},{17,145,273,401},{25,153,281,409},{33,1..., dimensions={0} | all-to-all | bytes 65536 | tf_op jit(solution)/shard_map/all_to_all | solution.py:243
  29.6 37.3 %all_to_all.42.recv_ref = f32[64,8,256]{2,1,0:T(8,128)S(1)} all-to-all(f32[64,8,256]{2,1,0:T(8,128)S(1)} %shard_map.53), channel_id=1, replica_groups={{1,9,17,25,33,41,49,57,65,73,81,89,97,105,113,121,129,137,145,153,161,1..., dimensions={0} | all-to-all | bytes 1048576 | tf_op jit(solution)/shard_map/all_to_all | solution.py:243
  66.9 2.3 %shard_map.54 = (f32[8,1024]{1,0:T(8,128)S(1)}, f32[4,8,2176]{2,1,0:T(8,128)S(1)}) custom-call(f32[64,8,256]{2,1,0:T(8,128)S(1)} %all_to_all.42.recv_ref, f32[8,1024]{1,0:T(8,128)S(1)} %get-tuple-element.33.w_ref, bf16[2048,512]{1,0:T(8,128)(2,1)S(1)} %get-tuple-element.34.high0, bf16[2048,512]{1,0:T(8,128)(2,1)S(1)} %get-tuple-element.35.low0, ...), custom_call_target="tpu_custom_call" | custom-call | tf_op jit(solution)/shard_map/pallas_call | solution.py:216
  69.2 9.4 %all_to_all.43.recv_ref = f32[4,8,2176]{2,1,0:T(8,128)S(1)} all-to-all(f32[4,8,2176]{2,1,0:T(8,128)S(1)} %get-tuple-element.36), channel_id=1, replica_groups={{1,3,5,7},{9,11,13,15},{17,19,21,23},{25,27,29,31},{33,35,37,39},{41,43..., dimensions={0} | all-to-all | bytes 557056 | tf_op jit(solution)/shard_map/all_to_all | solution.py:243
  78.6 1.2 shard_map.55
  79.8 8.6 %all_to_all.44.recv_ref = f32[4,8,256]{2,1,0:T(8,128)S(1)} all-to-all(f32[4,8,256]{2,1,0:T(8,128)S(1)} %get-tuple-element.38), channel_id=1, replica_groups={{1,129,257,385},{9,137,265,393},{17,145,273,401},{25,153,281,409},{33,1..., dimensions={0} | all-to-all | bytes 65536 | tf_op jit(solution)/shard_map/all_to_all | solution.py:243
  88.4 28.5 %all_to_all.45.recv_ref = f32[64,8,256]{2,1,0:T(8,128)S(1)} all-to-all(f32[64,8,256]{2,1,0:T(8,128)S(1)} %shard_map.56), channel_id=1, replica_groups={{1,9,17,25,33,41,49,57,65,73,81,89,97,105,113,121,129,137,145,153,161,1..., dimensions={0} | all-to-all | bytes 1048576 | tf_op jit(solution)/shard_map/all_to_all | solution.py:243
  116.9 2.3 %shard_map.57 = (f32[8,1024]{1,0:T(8,128)S(1)}, f32[4,8,2176]{2,1,0:T(8,128)S(1)}) custom-call(f32[64,8,256]{2,1,0:T(8,128)S(1)} %all_to_all.45.recv_ref, f32[8,1024]{1,0:T(8,128)S(1)} %get-tuple-element.39.resid_ref, bf16[2048,512]{1,0:T(8,128)(2,1)S(1)} %get-tuple-element.34.high0, bf16[2048,512]{1,0:T(8,128)(2,1)S(1)} %get-tuple-element.35.low0, ...), custom_call_target="tpu_custom_call" | custom-call | tf_op jit(solution)/shard_map/pallas_call | solution.py:216
  119.2 9.5 %all_to_all.46.recv_ref = f32[4,8,2176]{2,1,0:T(8,128)S(1)} all-to-all(f32[4,8,2176]{2,1,0:T(8,128)S(1)} %get-tuple-element.40), channel_id=1, replica_groups={{1,3,5,7},{9,11,13,15},{17,19,21,23},{25,27,29,31},{33,35,37,39},{41,43..., dimensions={0} | all-to-all | bytes 557056 | tf_op jit(solution)/shard_map/all_to_all | solution.py:243
  128.6 0.2 shard_map.58
  128.9 20.9 %all_to_all.47.curvature_ref = f32[64,1,128]{2,1,0:T(1,128)S(1)} all-to-all(f32[64,1,128]{2,1,0:T(1,128)S(1)} %get-tuple-element.43), channel_id=1, replica_groups={{1,9,17,25,33,41,49,57,65,73,81,89,97,105,113,121,129,137,145,153,161,1..., dimensions={0} | all-to-all | bytes 65536 | tf_op jit(solution)/shard_map/all_to_all | solution.py:243
  149.7 0.1 shard_map.59
  149.9 1.9 %all-gather.1 = f32[16,3072]{1,0:T(8,128)S(1)} all-gather(f32[8,3072]{1,0:T(8,128)S(1)} %shard_map.59), channel_id=3, replica_groups=mesh['x'=4,'z'=16,'y'=4,'core'=2] {'core'}, dimensions={0}, use_global_device_ids=true | all-gather | bytes 294912 | tf_op jit(solution)/shard_map/all_gather | solution.py:308
  151.8 0.6 shard_map.60
  (3 shorter events, 0.1 us)
Async XLA Ops:
  0.6 20.6 %copy-start = (s32[2048]{0:T(1024)S(1)}, s32[2048]{0:T(1024)}, u32[]{:S(2)}) copy-start(s32[2048]{0:T(1024)} %param.4) | copy-start | bytes 24580
  12.0 9.2 %collective-permute-start = (f32[2048,512]{1,0:T(8,128)S(1)}, f32[2048,512]{1,0:T(8,128)S(1)}, u32[]{:S(2)}, u32[]{:S(2)}) collective-permute-start(f32[2048,512]{1,0:T(8,128)S(1)} %get-tuple-element.29), channel_id=1, source_target_pairs={{0,1},{2,3},{4,5},{6,7},{8,9},{10,11},{12,13},{14,15},{16,17},{18,... | collective-permute-start | bytes 12582920 | tf_op jit(solution)/shard_map/ppermute | solution.py:280

commit v7 on v5

--- a/solution.py
+++ b/solution.py
@@ -117,21 +117,25 @@
     spread(out_ref, sum_first(recv_ref, 0, rows))
 
 
-def grad_kernel(
-    recv_ref, labels_ref, moved_ref, high1_ref, low1_ref,
-    logits_ref, probs_ref, out_ref, high0_ref, low0_ref,
-):
-    x = moved_ref[...]
-    high = x.astype(BF16)
-    high0_ref[...] = high
-    low0_ref[...] = (x - high.astype(F32)).astype(BF16)
+def grad_kernel(recv_ref, labels_ref, high1, low1, logits_ref, probs_ref, parts_ref, half_ref):
     logits = sum_first(recv_ref)
     logits_ref[...] = logits
     expo = jnp.exp(logits)
     probs = expo / jnp.sum(expo, axis=0, keepdims=True)
     probs_ref[...] = probs
     onehot = (labels_ref[...] == lax.broadcasted_iota(jnp.int32, logits.shape, 0)).astype(F32)
-    chip_columns(out_ref, probs - onehot, ((high0_ref, low0_ref), (high1_ref, low1_ref)))
+    parts = both_parts(probs - onehot)
+    parts_ref[...] = parts
+    half_ref[...] = product_of(parts, high1[...], low1[...], NN)
+
+
+def moved_kernel(parts_ref, half_ref, moved_ref, out_ref, high0_ref, low0_ref):
+    x = moved_ref[...]
+    high = x.astype(BF16)
+    high0_ref[...] = high
+    low0_ref[...] = (x - high.astype(F32)).astype(BF16)
+    first = product_of(parts_ref[...], high0_ref[...], low0_ref[...], NN)
+    spread_blocks(out_ref, jnp.concatenate([first, half_ref[...]], axis=1))
 
 
 def send_rows(out_ref, value, tile, parts_of):
@@ -168,7 +172,7 @@
 def scalars(rr0, tail):
     along, square = tail[:1, :1], tail[:1, 1:2]
     alpha = rr0 / along
-    rr1 = rr0 - 2.0 * alpha * along + alpha * alpha * square
+    rr1 = jnp.maximum(rr0 - 2.0 * alpha * along + alpha * alpha * square, 0.0)
     return alpha, rr1, rr1 / rr0
 
 
@@ -192,7 +196,8 @@
     rr0 = tail_ref[:1, :1]
     alpha, rr1, beta = scalars(rr0, tail2_ref[...])
     curvature = sum_first(curvature_ref)[:, :1]
-    alpha1 = rr1 / (curvature / count + RIDGE * (rr1 + beta * beta * rr0))
+    bent = curvature / count + RIDGE * (rr1 + beta * beta * rr0)
+    alpha1 = jnp.where(rr1 > 0.0, rr1 / bent, 0.0)
     resid = resid_ref[...]
     direction = resid - alpha * product_ref[...] + beta * resid
     out_ref[:, rows:] = w_ref[...] + (alpha * resid + alpha1 * direction)
@@ -278,11 +283,12 @@
     gathered, held = lax.optimization_barrier((lax.all_gather(partial, "core"), held))
     moved = lax.ppermute(held, "core", [(0, 1)])
     weights, partial = call(chip_kernel, [coeffs, (lines, *cells)], gathered)
-    logits, probs, partial, high0, low0 = call(
+    logits, probs, terms, half = call(
         grad_kernel,
-        [cells, cells, blocks, split, split],
-        exchange(partial, "y"), labels.reshape(1, rows), moved, high1, low1,
-    )
+        [cells, cells, pltpu.VMEM((2 * classes, rows), BF16), (classes, width)],
+        exchange(partial, "y"), labels.reshape(1, rows), high1, low1,
+    )
+    partial, high0, low0 = call(moved_kernel, [blocks, split, split], terms, half, moved)
     parts = (high0, low0, high1, low1)
     resid, partial = call(
         functools.partial(resid_kernel, count), [coeffs, padded], over_cells(partial), weights, *parts

time: 134 us -> 134 us (level)
    pallas_call x13 -> x14, Pallas kernels: 11.5 us -> 11.5 us  [call(): pl.pallas_call(kernel, out_shape=shapes, in_specs=in_specs or [vmem] * le...]
  transfers between devices with their start and end apart: 1 -> 1, of which waited for: 0 -> 0; matrix products, arithmetic and copies ran while one was open for 0% -> 0% of each run, Pallas kernels for 0% -> 1%
where the time goes in v7:
time: 134 us; the launch traced here: 133 us
  blocking collectives  120 us (90%)
  Pallas kernels  11.5 us (9%)
    all_to_all x10, blocking collectives, exchange(): lax.all_to_all(blocks, GRID, 0, 0, axis_index_groups=groups(kind), tiled=...  109 us
    pallas_call x14, Pallas kernels, call(): pl.pallas_call(kernel, out_shape=shapes, in_specs=in_specs or [vmem] * le...  11.5 us
    all_gather x1, blocking collectives, on_device(): lax.all_gather(partial, 'core')  8.4 us
  transfers between devices with their start and end apart: 1, of which 0 were waited for; matrix products, arithmetic and copies ran while one was open for 0% of the time, Pallas kernels for 1%

profile of v7, /device:TPU:1, one launch (start us, length us, event | category | flops | bytes accessed | tf_op | source)
XLA Modules:
  0.0 133.2 jit_solution(10580063284325304618)
XLA Ops:
  0.6 0.0 copy-start
  0.6 2.9 %shard_map.50 = (bf16[2048,512]{1,0:T(8,128)(2,1)S(1)}, bf16[2048,512]{1,0:T(8,128)(2,1)S(1)}, f32[8,2560]{1,0:T(8,128)S(1)}, f32[2048,512]{1,0:T(8,128)S(1)}) custom-call(f32[8,512]{1,0:T(8,128)} %w_ref.1, f32[2048,512]{1,0:T(8,128)} %x_ref.1), custom_call_target="tpu_custom_call" | custom-call | tf_op jit(solution)/shard_map/pallas_call | solution.py:217
  3.6 8.4 %all-gather = f32[16,2560]{1,0:T(8,128)S(1)} all-gather(f32[8,2560]{1,0:T(8,128)S(1)} %get-tuple-element.27), channel_id=2, replica_groups=mesh['x'=4,'z'=16,'y'=4,'core'=2] {'core'}, dimensions={0}, use_global_device_ids=true | all-gather | bytes 245760 | tf_op jit(solution)/shard_map/all_gather | solution.py:283
  12.0 1.3 collective-permute-start
  13.3 7.9 %all_to_all.50.recv_ref = f32[4,8,2048]{2,1,0:T(8,128)S(1)} all-to-all(f32[4,8,2048]{2,1,0:T(8,128)S(1)} %get-tuple-element.30), channel_id=1, replica_groups={{1,3,5,7},{9,11,13,15},{17,19,21,23},{25,27,29,31},{33,35,37,39},{41,43..., dimensions={0} | all-to-all | bytes 524288 | tf_op jit(solution)/shard_map/all_to_all | solution.py:244
  21.2 0.0 copy-done
  21.2 0.6 shard_map.52
  21.9 0.0 collective-permute-done.moved_ref
  21.9 1.1 shard_map.53
  23.0 6.7 %all_to_all.51.recv_ref = f32[4,8,256]{2,1,0:T(8,128)S(1)} all-to-all(f32[4,8,256]{2,1,0:T(8,128)S(1)} %get-tuple-element.36), channel_id=1, replica_groups={{1,129,257,385},{9,137,265,393},{17,145,273,401},{25,153,281,409},{33,1..., dimensions={0} | all-to-all | bytes 65536 | tf_op jit(solution)/shard_map/all_to_all | solution.py:244
  29.6 24.4 %all_to_all.52.recv_ref = f32[16,8,256]{2,1,0:T(8,128)S(1)} all-to-all(f32[16,8,256]{2,1,0:T(8,128)S(1)} %shard_map.54), channel_id=1, replica_groups={{1,9,17,25,33,41,49,57,65,73,81,89,97,105,113,121},{3,11,19,27,35,43,51..., dimensions={0} | all-to-all | bytes 262144 | tf_op jit(solution)/shard_map/all_to_all | solution.py:244
  54.0 6.7 %all_to_all.53.recv_ref = f32[4,8,256]{2,1,0:T(8,128)S(1)} all-to-all(f32[4,8,256]{2,1,0:T(8,128)S(1)} %shard_map.55), channel_id=1, replica_groups={{1,129,257,385},{9,137,265,393},{17,145,273,401},{25,153,281,409},{33,1..., dimensions={0} | all-to-all | bytes 65536 | tf_op jit(solution)/shard_map/all_to_all | solution.py:244
  60.7 2.3 %shard_map.56 = (f32[8,1024]{1,0:T(8,128)S(1)}, f32[4,8,2176]{2,1,0:T(8,128)S(1)}) custom-call(f32[4,8,256]{2,1,0:T(8,128)S(1)} %all_to_all.53.recv_ref, f32[8,1024]{1,0:T(8,128)S(1)} %get-tuple-element.37.w_ref, bf16[2048,512]{1,0:T(8,128)(2,1)S(1)} %get-tuple-element.38.high0, bf16[2048,512]{1,0:T(8,128)(2,1)S(1)} %get-tuple-element.39.low0, ...), custom_call_target="tpu_custom_call" | custom-call | tf_op jit(solution)/shard_map/pallas_call | solution.py:217
  63.0 8.0 %all_to_all.54.recv_ref = f32[4,8,2176]{2,1,0:T(8,128)S(1)} all-to-all(f32[4,8,2176]{2,1,0:T(8,128)S(1)} %get-tuple-element.40), channel_id=1, replica_groups={{1,3,5,7},{9,11,13,15},{17,19,21,23},{25,27,29,31},{33,35,37,39},{41,43..., dimensions={0} | all-to-all | bytes 557056 | tf_op jit(solution)/shard_map/all_to_all | solution.py:244
  70.9 1.2 shard_map.57
  72.1 6.7 %all_to_all.55.recv_ref = f32[4,8,256]{2,1,0:T(8,128)S(1)} all-to-all(f32[4,8,256]{2,1,0:T(8,128)S(1)} %get-tuple-element.42), channel_id=1, replica_groups={{1,129,257,385},{9,137,265,393},{17,145,273,401},{25,153,281,409},{33,1..., dimensions={0} | all-to-all | bytes 65536 | tf_op jit(solution)/shard_map/all_to_all | solution.py:244
  78.8 15.8 %all_to_all.56.recv_ref = f32[16,8,256]{2,1,0:T(8,128)S(1)} all-to-all(f32[16,8,256]{2,1,0:T(8,128)S(1)} %shard_map.58), channel_id=1, replica_groups={{1,9,17,25,33,41,49,57,65,73,81,89,97,105,113,121},{3,11,19,27,35,43,51..., dimensions={0} | all-to-all | bytes 262144 | tf_op jit(solution)/shard_map/all_to_all | solution.py:244
  94.6 7.1 %all_to_all.57.recv_ref = f32[4,8,256]{2,1,0:T(8,128)S(1)} all-to-all(f32[4,8,256]{2,1,0:T(8,128)S(1)} %shard_map.59), channel_id=1, replica_groups={{1,129,257,385},{9,137,265,393},{17,145,273,401},{25,153,281,409},{33,1..., dimensions={0} | all-to-all | bytes 65536 | tf_op jit(solution)/shard_map/all_to_all | solution.py:244
  101.7 2.3 %shard_map.60 = (f32[8,1024]{1,0:T(8,128)S(1)}, f32[4,8,2176]{2,1,0:T(8,128)S(1)}) custom-call(f32[4,8,256]{2,1,0:T(8,128)S(1)} %all_to_all.57.recv_ref, f32[8,1024]{1,0:T(8,128)S(1)} %get-tuple-element.43.resid_ref, bf16[2048,512]{1,0:T(8,128)(2,1)S(1)} %get-tuple-element.38.high0, bf16[2048,512]{1,0:T(8,128)(2,1)S(1)} %get-tuple-element.39.low0, ...), custom_call_target="tpu_custom_call" | custom-call | tf_op jit(solution)/shard_map/pallas_call | solution.py:217
  104.0 8.0 %all_to_all.58.recv_ref = f32[4,8,2176]{2,1,0:T(8,128)S(1)} all-to-all(f32[4,8,2176]{2,1,0:T(8,128)S(1)} %get-tuple-element.44), channel_id=1, replica_groups={{1,3,5,7},{9,11,13,15},{17,19,21,23},{25,27,29,31},{33,35,37,39},{41,43..., dimensions={0} | all-to-all | bytes 557056 | tf_op jit(solution)/shard_map/all_to_all | solution.py:244
  112.0 0.2 shard_map.61
  112.2 18.2 %all_to_all.59.curvature_ref = f32[64,1,128]{2,1,0:T(1,128)S(1)} all-to-all(f32[64,1,128]{2,1,0:T(1,128)S(1)} %get-tuple-element.47), channel_id=1, replica_groups={{1,9,17,25,33,41,49,57,65,73,81,89,97,105,113,121,129,137,145,153,161,1..., dimensions={0} | all-to-all | bytes 65536 | tf_op jit(solution)/shard_map/all_to_all | solution.py:244
  130.4 0.1 shard_map.62
  130.6 1.9 %all-gather.1 = f32[16,3072]{1,0:T(8,128)S(1)} all-gather(f32[8,3072]{1,0:T(8,128)S(1)} %shard_map.62), channel_id=3, replica_groups=mesh['x'=4,'z'=16,'y'=4,'core'=2] {'core'}, dimensions={0}, use_global_device_ids=true | all-gather | bytes 294912 | tf_op jit(solution)/shard_map/all_gather | solution.py:313
  132.5 0.6 shard_map.63
  (5 shorter events, 0.1 us)
Async XLA Ops:
  0.6 20.6 %copy-start = (s32[2048]{0:T(1024)S(1)}, s32[2048]{0:T(1024)}, u32[]{:S(2)}) copy-start(s32[2048]{0:T(1024)} %param.4) | copy-start | bytes 24580
  12.0 9.9 %collective-permute-start = (f32[2048,512]{1,0:T(8,128)S(1)}, f32[2048,512]{1,0:T(8,128)S(1)}, u32[]{:S(2)}, u32[]{:S(2)}) collective-permute-start(f32[2048,512]{1,0:T(8,128)S(1)} %get-tuple-element.35), channel_id=1, source_target_pairs={{0,1},{2,3},{4,5},{6,7},{8,9},{10,11},{12,13},{14,15},{16,17},{18,... | collective-permute-start | bytes 12582920 | tf_op jit(solution)/shard_map/ppermute | solution.py:284

commit v8 on v7

--- a/solution.py
+++ b/solution.py
@@ -53,9 +53,12 @@
     return jnp.sum(jnp.sum(value, axis=1, keepdims=True), axis=0, keepdims=True)
 
 
-def tile_of(first, second):
+def tile_of(*values):
     column = lax.broadcasted_iota(jnp.int32, (8, LANES), 1)
-    return jnp.where(column == 0, first, jnp.where(column == 1, second, 0.0))
+    tile = jnp.zeros((8, LANES), F32)
+    for i, value in enumerate(values):
+        tile = jnp.where(column == i, value, tile)
+    return tile
 
 
 def spread(ref, value):
@@ -138,49 +141,42 @@
     spread_blocks(out_ref, jnp.concatenate([first, half_ref[...]], axis=1))
 
 
-def send_rows(out_ref, value, tile, parts_of):
-    rows = out_ref.shape[2] - LANES
-    image = chip_rows(value, parts_of)
-    for i in range(out_ref.shape[0]):
-        out_ref[i, :, :rows] = image
-        out_ref[i, :, rows:] = tile
-
-
 def resid_kernel(count, recv_ref, w_ref, high0, low0, high1, low1, resid_ref, out_ref):
     resid = -(joined(recv_ref) / count + RIDGE * w_ref[...])
     resid_ref[...] = resid
-    tile = tile_of(total_of(resid * resid), 0.0)
-    send_rows(out_ref, resid, tile, ((high0, low0), (high1, low1)))
+    spread(out_ref, chip_rows(resid, ((high0, low0), (high1, low1))))
 
 
 def product_kernel(count, recv_ref, resid_ref, high0, low0, high1, low1, product_ref, out_ref):
     resid = resid_ref[...]
     product = joined(recv_ref) / count + RIDGE * resid
     product_ref[...] = product
-    tile = tile_of(total_of(resid * product), total_of(product * product))
-    send_rows(out_ref, product, tile, ((high0, low0), (high1, low1)))
-
-
-def image_kernel(recv_ref, probs_ref, high0, low0, high1, low1, image_ref, tail_ref, out_ref):
-    rows = image_ref.shape[1]
-    image = sum_first(recv_ref, 0, rows)
+    tile = tile_of(*(total_of(a * b) for a, b in ((resid, resid), (resid, product), (product, product))))
+    image = chip_rows(product, ((high0, low0), (high1, low1)))
+    rows = image.shape[1]
+    for i in range(out_ref.shape[0]):
+        out_ref[i, :, :rows] = image
+        out_ref[i, :, rows:] = tile
+
+
+def image_kernel(recv_ref, probs_ref, high0, low0, high1, low1, image_ref, out_ref):
+    image = sum_first(recv_ref)
     image_ref[...] = image
-    tail_ref[...] = sum_first(recv_ref, rows, rows + LANES)
     chip_columns(out_ref, curved(probs_ref[...], image), ((high0, low0), (high1, low1)))
 
 
-def scalars(rr0, tail):
-    along, square = tail[:1, :1], tail[:1, 1:2]
+def scalars(tail):
+    rr0, along, square = tail[:1, :1], tail[:1, 1:2], tail[:1, 2:3]
     alpha = rr0 / along
     rr1 = jnp.maximum(rr0 - 2.0 * alpha * along + alpha * alpha * square, 0.0)
-    return alpha, rr1, rr1 / rr0
-
-
-def second_kernel(recv_ref, tail_ref, probs_ref, image_ref, direction_ref, tail2_ref, out_ref):
+    return rr0, alpha, rr1, rr1 / rr0
+
+
+def second_kernel(recv_ref, probs_ref, image_ref, direction_ref, tail_ref, out_ref):
     rows = image_ref.shape[1]
     tail = sum_first(recv_ref, rows, rows + LANES)
-    tail2_ref[...] = tail
-    alpha, rr1, beta = scalars(tail_ref[:1, :1], tail)
+    tail_ref[...] = tail
+    rr0, alpha, rr1, beta = scalars(tail)
     image = image_ref[...]
     direction = image - alpha * sum_first(recv_ref, 0, rows) + beta * image
     direction_ref[...] = direction
@@ -189,12 +185,11 @@
 
 
 def last_kernel(
-    count, curvature_ref, tail_ref, tail2_ref, w_ref, resid_ref, product_ref, logits_ref,
+    count, curvature_ref, tail_ref, w_ref, resid_ref, product_ref, logits_ref,
     image_ref, direction_ref, out_ref,
 ):
     rows = logits_ref.shape[1]
-    rr0 = tail_ref[:1, :1]
-    alpha, rr1, beta = scalars(rr0, tail2_ref[...])
+    rr0, alpha, rr1, beta = scalars(tail_ref[...])
     curvature = sum_first(curvature_ref)[:, :1]
     bent = curvature / count + RIDGE * (rr1 + beta * beta * rr0)
     alpha1 = jnp.where(rr1 > 0.0, rr1 / bent, 0.0)
@@ -291,23 +286,23 @@
     partial, high0, low0 = call(moved_kernel, [blocks, split, split], terms, half, moved)
     parts = (high0, low0, high1, low1)
     resid, partial = call(
-        functools.partial(resid_kernel, count), [coeffs, padded], over_cells(partial), weights, *parts
-    )
-    image, tail, partial = call(
-        image_kernel, [cells, tile, blocks], exchange(partial, "y"), probs, *parts
+        functools.partial(resid_kernel, count), [coeffs, (lines, *cells)], over_cells(partial), weights, *parts
+    )
+    image, partial = call(
+        image_kernel, [cells, blocks], exchange(partial, "y"), probs, *parts
     )
     product, partial = call(
         functools.partial(product_kernel, count), [coeffs, padded], over_cells(partial), resid, *parts
     )
-    direction, tail2, curvature = call(
+    direction, tail, curvature = call(
         second_kernel,
         [cells, tile, (lax.axis_size(CELLS), 1, LANES)],
-        exchange(partial, "y"), tail, probs, image,
+        exchange(partial, "y"), probs, image,
     )
     (result,) = call(
         functools.partial(last_kernel, count),
         [(classes, rows + 2 * width)],
-        exchange(curvature, "cells"), tail, tail2, weights, resid, product, logits, image, direction,
+        exchange(curvature, "cells"), tail, weights, resid, product, logits, image, direction,
     )
     return tuple(
         call(share_kernel, [(classes, width), cells], lax.all_gather(result, "core"))

time: 134 us -> 134 us (level)
  no operation moved by 1% of the time
where the time goes in v8:
time: 134 us; the launch traced here: 133 us
  blocking collectives  120 us (90%)
  Pallas kernels  11.5 us (9%)
    all_to_all x10, blocking collectives, exchange(): lax.all_to_all(blocks, GRID, 0, 0, axis_index_groups=groups(kind), tiled=...  109 us
    pallas_call x14, Pallas kernels, call(): pl.pallas_call(kernel, out_shape=shapes, in_specs=in_specs or [vmem] * le...  11.5 us
    all_gather x1, blocking collectives, on_device(): lax.all_gather(partial, 'core')  8.4 us
  transfers between devices with their start and end apart: 1, of which 0 were waited for; matrix products, arithmetic and copies ran while one was open for 0% of the time, Pallas kernels for 1%

profile of v8, /device:TPU:1, one launch (start us, length us, event | category | flops | bytes accessed | tf_op | source)
XLA Modules:
  0.0 133.1 jit_solution(11910749734091379376)
XLA Ops:
  0.6 0.0 copy-start
  0.6 2.9 %shard_map.50 = (bf16[2048,512]{1,0:T(8,128)(2,1)S(1)}, bf16[2048,512]{1,0:T(8,128)(2,1)S(1)}, f32[8,2560]{1,0:T(8,128)S(1)}, f32[2048,512]{1,0:T(8,128)S(1)}) custom-call(f32[8,512]{1,0:T(8,128)} %w_ref.1, f32[2048,512]{1,0:T(8,128)} %x_ref.1), custom_call_target="tpu_custom_call" | custom-call | tf_op jit(solution)/shard_map/pallas_call | solution.py:212
  3.6 8.4 %all-gather = f32[16,2560]{1,0:T(8,128)S(1)} all-gather(f32[8,2560]{1,0:T(8,128)S(1)} %get-tuple-element.26), channel_id=2, replica_groups=mesh['x'=4,'z'=16,'y'=4,'core'=2] {'core'}, dimensions={0}, use_global_device_ids=true | all-gather | bytes 245760 | tf_op jit(solution)/shard_map/all_gather | solution.py:278
  12.0 1.3 collective-permute-start
  13.3 7.9 %all_to_all.50.recv_ref = f32[4,8,2048]{2,1,0:T(8,128)S(1)} all-to-all(f32[4,8,2048]{2,1,0:T(8,128)S(1)} %get-tuple-element.29), channel_id=1, replica_groups={{1,3,5,7},{9,11,13,15},{17,19,21,23},{25,27,29,31},{33,35,37,39},{41,43..., dimensions={0} | all-to-all | bytes 524288 | tf_op jit(solution)/shard_map/all_to_all | solution.py:239
  21.2 0.0 copy-done
  21.2 0.6 shard_map.52
  21.9 0.0 collective-permute-done.moved_ref
  21.9 1.1 shard_map.53
  22.9 6.7 %all_to_all.51.recv_ref = f32[4,8,256]{2,1,0:T(8,128)S(1)} all-to-all(f32[4,8,256]{2,1,0:T(8,128)S(1)} %get-tuple-element.35), channel_id=1, replica_groups={{1,129,257,385},{9,137,265,393},{17,145,273,401},{25,153,281,409},{33,1..., dimensions={0} | all-to-all | bytes 65536 | tf_op jit(solution)/shard_map/all_to_all | solution.py:239
  29.6 24.4 %all_to_all.52.recv_ref = f32[16,8,256]{2,1,0:T(8,128)S(1)} all-to-all(f32[16,8,256]{2,1,0:T(8,128)S(1)} %shard_map.54), channel_id=1, replica_groups={{1,9,17,25,33,41,49,57,65,73,81,89,97,105,113,121},{3,11,19,27,35,43,51..., dimensions={0} | all-to-all | bytes 262144 | tf_op jit(solution)/shard_map/all_to_all | solution.py:239
  54.0 6.7 %all_to_all.53.recv_ref = f32[4,8,256]{2,1,0:T(8,128)S(1)} all-to-all(f32[4,8,256]{2,1,0:T(8,128)S(1)} %shard_map.55), channel_id=1, replica_groups={{1,129,257,385},{9,137,265,393},{17,145,273,401},{25,153,281,409},{33,1..., dimensions={0} | all-to-all | bytes 65536 | tf_op jit(solution)/shard_map/all_to_all | solution.py:239
  60.6 2.3 %shard_map.56 = (f32[8,1024]{1,0:T(8,128)S(1)}, f32[4,8,2048]{2,1,0:T(8,128)S(1)}) custom-call(f32[4,8,256]{2,1,0:T(8,128)S(1)} %all_to_all.53.recv_ref, f32[8,1024]{1,0:T(8,128)S(1)} %get-tuple-element.36.w_ref, bf16[2048,512]{1,0:T(8,128)(2,1)S(1)} %get-tuple-element.37.high0, bf16[2048,512]{1,0:T(8,128)(2,1)S(1)} %get-tuple-element.38.low0, ...), custom_call_target="tpu_custom_call" | custom-call | tf_op jit(solution)/shard_map/pallas_call | solution.py:212
  62.9 7.9 %all_to_all.54.recv_ref = f32[4,8,2048]{2,1,0:T(8,128)S(1)} all-to-all(f32[4,8,2048]{2,1,0:T(8,128)S(1)} %get-tuple-element.39), channel_id=1, replica_groups={{1,3,5,7},{9,11,13,15},{17,19,21,23},{25,27,29,31},{33,35,37,39},{41,43..., dimensions={0} | all-to-all | bytes 524288 | tf_op jit(solution)/shard_map/all_to_all | solution.py:239
  70.8 1.2 shard_map.57
  72.0 6.7 %all_to_all.55.recv_ref = f32[4,8,256]{2,1,0:T(8,128)S(1)} all-to-all(f32[4,8,256]{2,1,0:T(8,128)S(1)} %get-tuple-element.41), channel_id=1, replica_groups={{1,129,257,385},{9,137,265,393},{17,145,273,401},{25,153,281,409},{33,1..., dimensions={0} | all-to-all | bytes 65536 | tf_op jit(solution)/shard_map/all_to_all | solution.py:239
  78.7 15.8 %all_to_all.56.recv_ref = f32[16,8,256]{2,1,0:T(8,128)S(1)} all-to-all(f32[16,8,256]{2,1,0:T(8,128)S(1)} %shard_map.58), channel_id=1, replica_groups={{1,9,17,25,33,41,49,57,65,73,81,89,97,105,113,121},{3,11,19,27,35,43,51..., dimensions={0} | all-to-all | bytes 262144 | tf_op jit(solution)/shard_map/all_to_all | solution.py:239
  94.5 7.1 %all_to_all.57.recv_ref = f32[4,8,256]{2,1,0:T(8,128)S(1)} all-to-all(f32[4,8,256]{2,1,0:T(8,128)S(1)} %shard_map.59), channel_id=1, replica_groups={{1,129,257,385},{9,137,265,393},{17,145,273,401},{25,153,281,409},{33,1..., dimensions={0} | all-to-all | bytes 65536 | tf_op jit(solution)/shard_map/all_to_all | solution.py:239
  101.6 2.3 %shard_map.60 = (f32[8,1024]{1,0:T(8,128)S(1)}, f32[4,8,2176]{2,1,0:T(8,128)S(1)}) custom-call(f32[4,8,256]{2,1,0:T(8,128)S(1)} %all_to_all.57.recv_ref, f32[8,1024]{1,0:T(8,128)S(1)} %get-tuple-element.42.resid_ref, bf16[2048,512]{1,0:T(8,128)(2,1)S(1)} %get-tuple-element.37.high0, bf16[2048,512]{1,0:T(8,128)(2,1)S(1)} %get-tuple-element.38.low0, ...), custom_call_target="tpu_custom_call" | custom-call | tf_op jit(solution)/shard_map/pallas_call | solution.py:212
  103.9 8.0 %all_to_all.58.recv_ref = f32[4,8,2176]{2,1,0:T(8,128)S(1)} all-to-all(f32[4,8,2176]{2,1,0:T(8,128)S(1)} %get-tuple-element.43), channel_id=1, replica_groups={{1,3,5,7},{9,11,13,15},{17,19,21,23},{25,27,29,31},{33,35,37,39},{41,43..., dimensions={0} | all-to-all | bytes 557056 | tf_op jit(solution)/shard_map/all_to_all | solution.py:239
  111.9 0.3 shard_map.61
  112.1 18.2 %all_to_all.59.curvature_ref = f32[64,1,128]{2,1,0:T(1,128)S(1)} all-to-all(f32[64,1,128]{2,1,0:T(1,128)S(1)} %get-tuple-element.45), channel_id=1, replica_groups={{1,9,17,25,33,41,49,57,65,73,81,89,97,105,113,121,129,137,145,153,161,1..., dimensions={0} | all-to-all | bytes 65536 | tf_op jit(solution)/shard_map/all_to_all | solution.py:239
  130.3 0.1 shard_map.62
  130.5 1.9 %all-gather.1 = f32[16,3072]{1,0:T(8,128)S(1)} all-gather(f32[8,3072]{1,0:T(8,128)S(1)} %shard_map.62), channel_id=3, replica_groups=mesh['x'=4,'z'=16,'y'=4,'core'=2] {'core'}, dimensions={0}, use_global_device_ids=true | all-gather | bytes 294912 | tf_op jit(solution)/shard_map/all_gather | solution.py:308
  132.4 0.6 shard_map.63
  (5 shorter events, 0.1 us)
Async XLA Ops:
  0.6 20.6 %copy-start = (s32[2048]{0:T(1024)S(1)}, s32[2048]{0:T(1024)}, u32[]{:S(2)}) copy-start(s32[2048]{0:T(1024)} %param.4) | copy-start | bytes 24580
  12.0 9.9 %collective-permute-start = (f32[2048,512]{1,0:T(8,128)S(1)}, f32[2048,512]{1,0:T(8,128)S(1)}, u32[]{:S(2)}, u32[]{:S(2)}) collective-permute-start(f32[2048,512]{1,0:T(8,128)S(1)} %get-tuple-element.34), channel_id=1, source_target_pairs={{0,1},{2,3},{4,5},{6,7},{8,9},{10,11},{12,13},{14,15},{16,17},{18,... | collective-permute-start | bytes 12582920 | tf_op jit(solution)/shard_map/ppermute | solution.py:279

commit v9 on v7

--- a/solution.py
+++ b/solution.py
@@ -234,7 +234,8 @@
     elif kind == "y":
         pair = work.reshape(-1, ny), near.transpose(1, 2, 0).reshape(-1, nx)
     elif kind == "z":
-        pair = work.transpose(0, 2, 1).reshape(-1, nz), xyz.reshape(-1, nx * ny)
+        order = np.arange(nz) * 7 % nz
+        pair = work[:, order].transpose(0, 2, 1).reshape(-1, nz), xyz.reshape(-1, nx * ny)
     else:
         pair = work.transpose(2, 0, 1).reshape(ny, -1), xyz.reshape(ny, -1)
     return np.concatenate(pair).tolist()

time: 134 us -> 134 us (level)
  no operation moved by 1% of the time
where the time goes in v9:
time: 134 us; the launch traced here: 133 us
  blocking collectives  120 us (90%)
  Pallas kernels  11.5 us (9%)
    all_to_all x10, blocking collectives, exchange(): lax.all_to_all(blocks, GRID, 0, 0, axis_index_groups=groups(kind), tiled=...  109 us
    pallas_call x14, Pallas kernels, call(): pl.pallas_call(kernel, out_shape=shapes, in_specs=in_specs or [vmem] * le...  11.5 us
    all_gather x1, blocking collectives, on_device(): lax.all_gather(partial, 'core')  8.4 us
  transfers between devices with their start and end apart: 1, of which 0 were waited for; matrix products, arithmetic and copies ran while one was open for 0% of the time, Pallas kernels for 1%

profile of v9, /device:TPU:1, one launch (start us, length us, event | category | flops | bytes accessed | tf_op | source)
XLA Modules:
  0.0 133.3 jit_solution(8804345745913373568)
XLA Ops:
  0.6 0.0 copy-start
  0.6 2.9 %shard_map.50 = (bf16[2048,512]{1,0:T(8,128)(2,1)S(1)}, bf16[2048,512]{1,0:T(8,128)(2,1)S(1)}, f32[8,2560]{1,0:T(8,128)S(1)}, f32[2048,512]{1,0:T(8,128)S(1)}) custom-call(f32[8,512]{1,0:T(8,128)} %w_ref.1, f32[2048,512]{1,0:T(8,128)} %x_ref.1), custom_call_target="tpu_custom_call" | custom-call | tf_op jit(solution)/shard_map/pallas_call | solution.py:217
  3.6 8.4 %all-gather = f32[16,2560]{1,0:T(8,128)S(1)} all-gather(f32[8,2560]{1,0:T(8,128)S(1)} %get-tuple-element.27), channel_id=2, replica_groups=mesh['x'=4,'z'=16,'y'=4,'core'=2] {'core'}, dimensions={0}, use_global_device_ids=true | all-gather | bytes 245760 | tf_op jit(solution)/shard_map/all_gather | solution.py:284
  12.0 1.3 collective-permute-start
  13.3 7.9 %all_to_all.50.recv_ref = f32[4,8,2048]{2,1,0:T(8,128)S(1)} all-to-all(f32[4,8,2048]{2,1,0:T(8,128)S(1)} %get-tuple-element.30), channel_id=1, replica_groups={{1,3,5,7},{9,11,13,15},{17,19,21,23},{25,27,29,31},{33,35,37,39},{41,43..., dimensions={0} | all-to-all | bytes 524288 | tf_op jit(solution)/shard_map/all_to_all | solution.py:245
  21.2 0.0 copy-done
  21.2 0.6 shard_map.52
  21.9 0.0 collective-permute-done.moved_ref
  21.9 1.1 shard_map.53
  23.0 6.7 %all_to_all.51.recv_ref = f32[4,8,256]{2,1,0:T(8,128)S(1)} all-to-all(f32[4,8,256]{2,1,0:T(8,128)S(1)} %get-tuple-element.36), channel_id=1, replica_groups={{1,129,257,385},{9,137,265,393},{17,145,273,401},{25,153,281,409},{33,1..., dimensions={0} | all-to-all | bytes 65536 | tf_op jit(solution)/shard_map/all_to_all | solution.py:245
  29.6 24.3 %all_to_all.52.recv_ref = f32[16,8,256]{2,1,0:T(8,128)S(1)} all-to-all(f32[16,8,256]{2,1,0:T(8,128)S(1)} %shard_map.54), channel_id=1, replica_groups={{1,57,113,41,97,25,81,9,65,121,49,105,33,89,17,73},{3,59,115,43,99,27,8..., dimensions={0} | all-to-all | bytes 262144 | tf_op jit(solution)/shard_map/all_to_all | solution.py:245
  53.9 6.7 %all_to_all.53.recv_ref = f32[4,8,256]{2,1,0:T(8,128)S(1)} all-to-all(f32[4,8,256]{2,1,0:T(8,128)S(1)} %shard_map.55), channel_id=1, replica_groups={{1,129,257,385},{9,137,265,393},{17,145,273,401},{25,153,281,409},{33,1..., dimensions={0} | all-to-all | bytes 65536 | tf_op jit(solution)/shard_map/all_to_all | solution.py:245
  60.6 2.3 %shard_map.56 = (f32[8,1024]{1,0:T(8,128)S(1)}, f32[4,8,2176]{2,1,0:T(8,128)S(1)}) custom-call(f32[4,8,256]{2,1,0:T(8,128)S(1)} %all_to_all.53.recv_ref, f32[8,1024]{1,0:T(8,128)S(1)} %get-tuple-element.37.w_ref, bf16[2048,512]{1,0:T(8,128)(2,1)S(1)} %get-tuple-element.38.high0, bf16[2048,512]{1,0:T(8,128)(2,1)S(1)} %get-tuple-element.39.low0, ...), custom_call_target="tpu_custom_call" | custom-call | tf_op jit(solution)/shard_map/pallas_call | solution.py:217
  62.8 8.0 %all_to_all.54.recv_ref = f32[4,8,2176]{2,1,0:T(8,128)S(1)} all-to-all(f32[4,8,2176]{2,1,0:T(8,128)S(1)} %get-tuple-element.40), channel_id=1, replica_groups={{1,3,5,7},{9,11,13,15},{17,19,21,23},{25,27,29,31},{33,35,37,39},{41,43..., dimensions={0} | all-to-all | bytes 557056 | tf_op jit(solution)/shard_map/all_to_all | solution.py:245
  70.8 1.2 shard_map.57
  72.0 6.7 %all_to_all.55.recv_ref = f32[4,8,256]{2,1,0:T(8,128)S(1)} all-to-all(f32[4,8,256]{2,1,0:T(8,128)S(1)} %get-tuple-element.42), channel_id=1, replica_groups={{1,129,257,385},{9,137,265,393},{17,145,273,401},{25,153,281,409},{33,1..., dimensions={0} | all-to-all | bytes 65536 | tf_op jit(solution)/shard_map/all_to_all | solution.py:245
  78.7 15.9 %all_to_all.56.recv_ref = f32[16,8,256]{2,1,0:T(8,128)S(1)} all-to-all(f32[16,8,256]{2,1,0:T(8,128)S(1)} %shard_map.58), channel_id=1, replica_groups={{1,57,113,41,97,25,81,9,65,121,49,105,33,89,17,73},{3,59,115,43,99,27,8..., dimensions={0} | all-to-all | bytes 262144 | tf_op jit(solution)/shard_map/all_to_all | solution.py:245
  94.6 7.1 %all_to_all.57.recv_ref = f32[4,8,256]{2,1,0:T(8,128)S(1)} all-to-all(f32[4,8,256]{2,1,0:T(8,128)S(1)} %shard_map.59), channel_id=1, replica_groups={{1,129,257,385},{9,137,265,393},{17,145,273,401},{25,153,281,409},{33,1..., dimensions={0} | all-to-all | bytes 65536 | tf_op jit(solution)/shard_map/all_to_all | solution.py:245
  101.7 2.3 %shard_map.60 = (f32[8,1024]{1,0:T(8,128)S(1)}, f32[4,8,2176]{2,1,0:T(8,128)S(1)}) custom-call(f32[4,8,256]{2,1,0:T(8,128)S(1)} %all_to_all.57.recv_ref, f32[8,1024]{1,0:T(8,128)S(1)} %get-tuple-element.43.resid_ref, bf16[2048,512]{1,0:T(8,128)(2,1)S(1)} %get-tuple-element.38.high0, bf16[2048,512]{1,0:T(8,128)(2,1)S(1)} %get-tuple-element.39.low0, ...), custom_call_target="tpu_custom_call" | custom-call | tf_op jit(solution)/shard_map/pallas_call | solution.py:217
  104.0 8.0 %all_to_all.58.recv_ref = f32[4,8,2176]{2,1,0:T(8,128)S(1)} all-to-all(f32[4,8,2176]{2,1,0:T(8,128)S(1)} %get-tuple-element.44), channel_id=1, replica_groups={{1,3,5,7},{9,11,13,15},{17,19,21,23},{25,27,29,31},{33,35,37,39},{41,43..., dimensions={0} | all-to-all | bytes 557056 | tf_op jit(solution)/shard_map/all_to_all | solution.py:245
  112.0 0.2 shard_map.61
  112.2 18.3 %all_to_all.59.curvature_ref = f32[64,1,128]{2,1,0:T(1,128)S(1)} all-to-all(f32[64,1,128]{2,1,0:T(1,128)S(1)} %get-tuple-element.47), channel_id=1, replica_groups={{1,9,17,25,33,41,49,57,65,73,81,89,97,105,113,121,129,137,145,153,161,1..., dimensions={0} | all-to-all | bytes 65536 | tf_op jit(solution)/shard_map/all_to_all | solution.py:245
  130.5 0.1 shard_map.62
  130.7 1.9 %all-gather.1 = f32[16,3072]{1,0:T(8,128)S(1)} all-gather(f32[8,3072]{1,0:T(8,128)S(1)} %shard_map.62), channel_id=3, replica_groups=mesh['x'=4,'z'=16,'y'=4,'core'=2] {'core'}, dimensions={0}, use_global_device_ids=true | all-gather | bytes 294912 | tf_op jit(solution)/shard_map/all_gather | solution.py:314
  132.6 0.6 shard_map.63
  (5 shorter events, 0.1 us)
Async XLA Ops:
  0.6 20.6 %copy-start = (s32[2048]{0:T(1024)S(1)}, s32[2048]{0:T(1024)}, u32[]{:S(2)}) copy-start(s32[2048]{0:T(1024)} %param.4) | copy-start | bytes 24580
  12.0 9.9 %collective-permute-start = (f32[2048,512]{1,0:T(8,128)S(1)}, f32[2048,512]{1,0:T(8,128)S(1)}, u32[]{:S(2)}, u32[]{:S(2)}) collective-permute-start(f32[2048,512]{1,0:T(8,128)S(1)} %get-tuple-element.35), channel_id=1, source_target_pairs={{0,1},{2,3},{4,5},{6,7},{8,9},{10,11},{12,13},{14,15},{16,17},{18,... | collective-permute-start | bytes 12582920 | tf_op jit(solution)/shard_map/ppermute | solution.py:285

commit v10 on v7

--- a/solution.py
+++ b/solution.py
@@ -204,21 +204,25 @@
     out_ref[:, :rows] = logits_ref[...] + (alpha * image_ref[...] + alpha1 * direction_ref[...])
 
 
-def share_kernel(recv_ref, weights_ref, scores_ref):
+def share_kernel(recv_ref, weights_ref, scores_ref, sems):
     rows, width = scores_ref.shape[1], weights_ref.shape[1]
-    scores_ref[...] = recv_ref[1, :, :rows]
     start = pl.multiple_of(rows + width * lax.axis_index("core"), LANES)
-    weights_ref[...] = recv_ref[1, :, pl.ds(start, width)]
-
-
-def call(kernel, shapes, *args, in_specs=None, scratch=(), limit=4):
+    scores = pltpu.make_async_copy(recv_ref.at[1, :, pl.ds(0, rows)], scores_ref, sems.at[0])
+    weights = pltpu.make_async_copy(recv_ref.at[1, :, pl.ds(start, width)], weights_ref, sems.at[1])
+    scores.start()
+    weights.start()
+    scores.wait()
+    weights.wait()
+
+
+def call(kernel, shapes, *args, in_specs=None, space=pltpu.VMEM, scratch=(), limit=4):
     shapes = [jax.ShapeDtypeStruct(s, F32) if isinstance(s, tuple) else s for s in shapes]
     vmem = pl.BlockSpec(memory_space=pltpu.VMEM)
     return pl.pallas_call(
         kernel,
         out_shape=shapes,
         in_specs=in_specs or [vmem] * len(args),
-        out_specs=[vmem] * len(shapes),
+        out_specs=[pl.BlockSpec(memory_space=space)] * len(shapes),
         scratch_shapes=list(scratch),
         compiler_params=pltpu.CompilerParams(vmem_limit_bytes=limit * 1024 * 1024),
     )(*args)
@@ -310,7 +314,13 @@
         exchange(curvature, "cells"), tail, tail2, weights, resid, product, logits, image, direction,
     )
     return tuple(
-        call(share_kernel, [(classes, width), cells], lax.all_gather(result, "core"))
+        call(
+            share_kernel,
+            [(classes, width), cells],
+            lax.all_gather(result, "core"),
+            space=pltpu.HBM,
+            scratch=[pltpu.SemaphoreType.DMA((2,))],
+        )
     )
 
 

time: 134 us -> 134 us (level)
  no operation moved by 1% of the time
where the time goes in v10:
time: 134 us; the launch traced here: 133 us
  blocking collectives  120 us (90%)
  Pallas kernels  11.5 us (9%)
    all_to_all x10, blocking collectives, exchange(): lax.all_to_all(blocks, GRID, 0, 0, axis_index_groups=groups(kind), tiled=...  109 us
    pallas_call x14, Pallas kernels, call(): pl.pallas_call(kernel, out_shape=shapes, in_specs=in_specs or [vmem] * le...  11.5 us
    all_gather x1, blocking collectives, on_device(): lax.all_gather(partial, 'core')  8.4 us
  transfers between devices with their start and end apart: 1, of which 0 were waited for; matrix products, arithmetic and copies ran while one was open for 0% of the time, Pallas kernels for 1%

profile of v10, /device:TPU:1, one launch (start us, length us, event | category | flops | bytes accessed | tf_op | source)
XLA Modules:
  0.0 133.2 jit_solution(12866521463012531143)
XLA Ops:
  0.6 0.0 copy-start
  0.6 2.9 %shard_map.50 = (bf16[2048,512]{1,0:T(8,128)(2,1)S(1)}, bf16[2048,512]{1,0:T(8,128)(2,1)S(1)}, f32[8,2560]{1,0:T(8,128)S(1)}, f32[2048,512]{1,0:T(8,128)S(1)}) custom-call(f32[8,512]{1,0:T(8,128)} %w_ref.1, f32[2048,512]{1,0:T(8,128)} %x_ref.1), custom_call_target="tpu_custom_call" | custom-call | tf_op jit(solution)/shard_map/pallas_call | solution.py:221
  3.6 8.4 %all-gather = f32[16,2560]{1,0:T(8,128)S(1)} all-gather(f32[8,2560]{1,0:T(8,128)S(1)} %get-tuple-element.27), channel_id=2, replica_groups=mesh['x'=4,'z'=16,'y'=4,'core'=2] {'core'}, dimensions={0}, use_global_device_ids=true | all-gather | bytes 245760 | tf_op jit(solution)/shard_map/all_gather | solution.py:287
  12.0 1.3 collective-permute-start
  13.3 7.9 %all_to_all.50.recv_ref = f32[4,8,2048]{2,1,0:T(8,128)S(1)} all-to-all(f32[4,8,2048]{2,1,0:T(8,128)S(1)} %get-tuple-element.30), channel_id=1, replica_groups={{1,3,5,7},{9,11,13,15},{17,19,21,23},{25,27,29,31},{33,35,37,39},{41,43..., dimensions={0} | all-to-all | bytes 524288 | tf_op jit(solution)/shard_map/all_to_all | solution.py:248
  21.2 0.0 copy-done
  21.2 0.6 shard_map.52
  21.9 0.0 collective-permute-done.moved_ref
  21.9 1.1 shard_map.53
  23.0 6.7 %all_to_all.51.recv_ref = f32[4,8,256]{2,1,0:T(8,128)S(1)} all-to-all(f32[4,8,256]{2,1,0:T(8,128)S(1)} %get-tuple-element.36), channel_id=1, replica_groups={{1,129,257,385},{9,137,265,393},{17,145,273,401},{25,153,281,409},{33,1..., dimensions={0} | all-to-all | bytes 65536 | tf_op jit(solution)/shard_map/all_to_all | solution.py:248
  29.6 24.4 %all_to_all.52.recv_ref = f32[16,8,256]{2,1,0:T(8,128)S(1)} all-to-all(f32[16,8,256]{2,1,0:T(8,128)S(1)} %shard_map.54), channel_id=1, replica_groups={{1,9,17,25,33,41,49,57,65,73,81,89,97,105,113,121},{3,11,19,27,35,43,51..., dimensions={0} | all-to-all | bytes 262144 | tf_op jit(solution)/shard_map/all_to_all | solution.py:248
  54.0 6.7 %all_to_all.53.recv_ref = f32[4,8,256]{2,1,0:T(8,128)S(1)} all-to-all(f32[4,8,256]{2,1,0:T(8,128)S(1)} %shard_map.55), channel_id=1, replica_groups={{1,129,257,385},{9,137,265,393},{17,145,273,401},{25,153,281,409},{33,1..., dimensions={0} | all-to-all | bytes 65536 | tf_op jit(solution)/shard_map/all_to_all | solution.py:248
  60.7 2.3 %shard_map.56 = (f32[8,1024]{1,0:T(8,128)S(1)}, f32[4,8,2176]{2,1,0:T(8,128)S(1)}) custom-call(f32[4,8,256]{2,1,0:T(8,128)S(1)} %all_to_all.53.recv_ref, f32[8,1024]{1,0:T(8,128)S(1)} %get-tuple-element.37.w_ref, bf16[2048,512]{1,0:T(8,128)(2,1)S(1)} %get-tuple-element.38.high0, bf16[2048,512]{1,0:T(8,128)(2,1)S(1)} %get-tuple-element.39.low0, ...), custom_call_target="tpu_custom_call" | custom-call | tf_op jit(solution)/shard_map/pallas_call | solution.py:221
  63.0 8.0 %all_to_all.54.recv_ref = f32[4,8,2176]{2,1,0:T(8,128)S(1)} all-to-all(f32[4,8,2176]{2,1,0:T(8,128)S(1)} %get-tuple-element.40), channel_id=1, replica_groups={{1,3,5,7},{9,11,13,15},{17,19,21,23},{25,27,29,31},{33,35,37,39},{41,43..., dimensions={0} | all-to-all | bytes 557056 | tf_op jit(solution)/shard_map/all_to_all | solution.py:248
  70.9 1.2 shard_map.57
  72.1 6.7 %all_to_all.55.recv_ref = f32[4,8,256]{2,1,0:T(8,128)S(1)} all-to-all(f32[4,8,256]{2,1,0:T(8,128)S(1)} %get-tuple-element.42), channel_id=1, replica_groups={{1,129,257,385},{9,137,265,393},{17,145,273,401},{25,153,281,409},{33,1..., dimensions={0} | all-to-all | bytes 65536 | tf_op jit(solution)/shard_map/all_to_all | solution.py:248
  78.8 15.8 %all_to_all.56.recv_ref = f32[16,8,256]{2,1,0:T(8,128)S(1)} all-to-all(f32[16,8,256]{2,1,0:T(8,128)S(1)} %shard_map.58), channel_id=1, replica_groups={{1,9,17,25,33,41,49,57,65,73,81,89,97,105,113,121},{3,11,19,27,35,43,51..., dimensions={0} | all-to-all | bytes 262144 | tf_op jit(solution)/shard_map/all_to_all | solution.py:248
  94.6 7.1 %all_to_all.57.recv_ref = f32[4,8,256]{2,1,0:T(8,128)S(1)} all-to-all(f32[4,8,256]{2,1,0:T(8,128)S(1)} %shard_map.59), channel_id=1, replica_groups={{1,129,257,385},{9,137,265,393},{17,145,273,401},{25,153,281,409},{33,1..., dimensions={0} | all-to-all | bytes 65536 | tf_op jit(solution)/shard_map/all_to_all | solution.py:248
  101.7 2.3 %shard_map.60 = (f32[8,1024]{1,0:T(8,128)S(1)}, f32[4,8,2176]{2,1,0:T(8,128)S(1)}) custom-call(f32[4,8,256]{2,1,0:T(8,128)S(1)} %all_to_all.57.recv_ref, f32[8,1024]{1,0:T(8,128)S(1)} %get-tuple-element.43.resid_ref, bf16[2048,512]{1,0:T(8,128)(2,1)S(1)} %get-tuple-element.38.high0, bf16[2048,512]{1,0:T(8,128)(2,1)S(1)} %get-tuple-element.39.low0, ...), custom_call_target="tpu_custom_call" | custom-call | tf_op jit(solution)/shard_map/pallas_call | solution.py:221
  104.0 8.0 %all_to_all.58.recv_ref = f32[4,8,2176]{2,1,0:T(8,128)S(1)} all-to-all(f32[4,8,2176]{2,1,0:T(8,128)S(1)} %get-tuple-element.44), channel_id=1, replica_groups={{1,3,5,7},{9,11,13,15},{17,19,21,23},{25,27,29,31},{33,35,37,39},{41,43..., dimensions={0} | all-to-all | bytes 557056 | tf_op jit(solution)/shard_map/all_to_all | solution.py:248
  112.0 0.2 shard_map.61
  112.2 18.2 %all_to_all.59.curvature_ref = f32[64,1,128]{2,1,0:T(1,128)S(1)} all-to-all(f32[64,1,128]{2,1,0:T(1,128)S(1)} %get-tuple-element.47), channel_id=1, replica_groups={{1,9,17,25,33,41,49,57,65,73,81,89,97,105,113,121,129,137,145,153,161,1..., dimensions={0} | all-to-all | bytes 65536 | tf_op jit(solution)/shard_map/all_to_all | solution.py:248
  130.4 0.1 shard_map.62
  130.6 1.9 %all-gather.1 = f32[16,3072]{1,0:T(8,128)S(1)} all-gather(f32[8,3072]{1,0:T(8,128)S(1)} %shard_map.62), channel_id=3, replica_groups=mesh['x'=4,'z'=16,'y'=4,'core'=2] {'core'}, dimensions={0}, use_global_device_ids=true | all-gather | bytes 294912 | tf_op jit(solution)/shard_map/all_gather | solution.py:320
  132.5 0.6 shard_map.63
  (5 shorter events, 0.1 us)
Async XLA Ops:
  0.6 20.6 %copy-start = (s32[2048]{0:T(1024)S(1)}, s32[2048]{0:T(1024)}, u32[]{:S(2)}) copy-start(s32[2048]{0:T(1024)} %param.4) | copy-start | bytes 24580
  12.0 9.9 %collective-permute-start = (f32[2048,512]{1,0:T(8,128)S(1)}, f32[2048,512]{1,0:T(8,128)S(1)}, u32[]{:S(2)}, u32[]{:S(2)}) collective-permute-start(f32[2048,512]{1,0:T(8,128)S(1)} %get-tuple-element.35), channel_id=1, source_target_pairs={{0,1},{2,3},{4,5},{6,7},{8,9},{10,11},{12,13},{14,15},{16,17},{18,... | collective-permute-start | bytes 12582920 | tf_op jit(solution)/shard_map/ppermute | solution.py:288

commit v11 on v7

--- a/solution.py
+++ b/solution.py
@@ -13,7 +13,7 @@
 GRID = ("x", "z", "y", "core")
 FEAT = ("y", "core")
 LANES = 128
-CHUNK = 512
+CHUNK = 1024
 F32 = jnp.float32
 BF16 = jnp.bfloat16
 NN = (((1,), (0,)), ((), ()))

time: 134 us -> 134 us (level)
  no operation moved by 1% of the time
where the time goes in v11:
time: 134 us; the launch traced here: 133 us
  blocking collectives  120 us (90%)
  Pallas kernels  11.6 us (9%)
    all_to_all x10, blocking collectives, exchange(): lax.all_to_all(blocks, GRID, 0, 0, axis_index_groups=groups(kind), tiled=...  109 us
    pallas_call x14, Pallas kernels, call(): pl.pallas_call(kernel, out_shape=shapes, in_specs=in_specs or [vmem] * le...  11.6 us
    all_gather x1, blocking collectives, on_device(): lax.all_gather(partial, 'core')  8.4 us
  transfers between devices with their start and end apart: 1, of which 0 were waited for; matrix products, arithmetic and copies ran while one was open for 0% of the time, Pallas kernels for 1%

profile of v11, /device:TPU:1, one launch (start us, length us, event | category | flops | bytes accessed | tf_op | source)
XLA Modules:
  0.0 133.3 jit_solution(11847716861646150022)
XLA Ops:
  0.6 0.0 copy-start
  0.6 3.0 %shard_map.50 = (bf16[2048,512]{1,0:T(8,128)(2,1)S(1)}, bf16[2048,512]{1,0:T(8,128)(2,1)S(1)}, f32[8,2560]{1,0:T(8,128)S(1)}, f32[2048,512]{1,0:T(8,128)S(1)}) custom-call(f32[8,512]{1,0:T(8,128)} %w_ref.1, f32[2048,512]{1,0:T(8,128)} %x_ref.1), custom_call_target="tpu_custom_call" | custom-call | tf_op jit(solution)/shard_map/pallas_call | solution.py:217
  3.7 8.4 %all-gather = f32[16,2560]{1,0:T(8,128)S(1)} all-gather(f32[8,2560]{1,0:T(8,128)S(1)} %get-tuple-element.27), channel_id=2, replica_groups=mesh['x'=4,'z'=16,'y'=4,'core'=2] {'core'}, dimensions={0}, use_global_device_ids=true | all-gather | bytes 245760 | tf_op jit(solution)/shard_map/all_gather | solution.py:283
  12.1 1.3 collective-permute-start
  13.4 7.9 %all_to_all.50.recv_ref = f32[4,8,2048]{2,1,0:T(8,128)S(1)} all-to-all(f32[4,8,2048]{2,1,0:T(8,128)S(1)} %get-tuple-element.30), channel_id=1, replica_groups={{1,3,5,7},{9,11,13,15},{17,19,21,23},{25,27,29,31},{33,35,37,39},{41,43..., dimensions={0} | all-to-all | bytes 524288 | tf_op jit(solution)/shard_map/all_to_all | solution.py:244
  21.3 0.0 copy-done
  21.3 0.6 shard_map.52
  22.0 0.0 collective-permute-done.moved_ref
  22.0 1.1 shard_map.53
  23.1 6.7 %all_to_all.51.recv_ref = f32[4,8,256]{2,1,0:T(8,128)S(1)} all-to-all(f32[4,8,256]{2,1,0:T(8,128)S(1)} %get-tuple-element.36), channel_id=1, replica_groups={{1,129,257,385},{9,137,265,393},{17,145,273,401},{25,153,281,409},{33,1..., dimensions={0} | all-to-all | bytes 65536 | tf_op jit(solution)/shard_map/all_to_all | solution.py:244
  29.7 24.4 %all_to_all.52.recv_ref = f32[16,8,256]{2,1,0:T(8,128)S(1)} all-to-all(f32[16,8,256]{2,1,0:T(8,128)S(1)} %shard_map.54), channel_id=1, replica_groups={{1,9,17,25,33,41,49,57,65,73,81,89,97,105,113,121},{3,11,19,27,35,43,51..., dimensions={0} | all-to-all | bytes 262144 | tf_op jit(solution)/shard_map/all_to_all | solution.py:244
  54.1 6.7 %all_to_all.53.recv_ref = f32[4,8,256]{2,1,0:T(8,128)S(1)} all-to-all(f32[4,8,256]{2,1,0:T(8,128)S(1)} %shard_map.55), channel_id=1, replica_groups={{1,129,257,385},{9,137,265,393},{17,145,273,401},{25,153,281,409},{33,1..., dimensions={0} | all-to-all | bytes 65536 | tf_op jit(solution)/shard_map/all_to_all | solution.py:244
  60.8 2.3 %shard_map.56 = (f32[8,1024]{1,0:T(8,128)S(1)}, f32[4,8,2176]{2,1,0:T(8,128)S(1)}) custom-call(f32[4,8,256]{2,1,0:T(8,128)S(1)} %all_to_all.53.recv_ref, f32[8,1024]{1,0:T(8,128)S(1)} %get-tuple-element.37.w_ref, bf16[2048,512]{1,0:T(8,128)(2,1)S(1)} %get-tuple-element.38.high0, bf16[2048,512]{1,0:T(8,128)(2,1)S(1)} %get-tuple-element.39.low0, ...), custom_call_target="tpu_custom_call" | custom-call | tf_op jit(solution)/shard_map/pallas_call | solution.py:217
  63.1 8.0 %all_to_all.54.recv_ref = f32[4,8,2176]{2,1,0:T(8,128)S(1)} all-to-all(f32[4,8,2176]{2,1,0:T(8,128)S(1)} %get-tuple-element.40), channel_id=1, replica_groups={{1,3,5,7},{9,11,13,15},{17,19,21,23},{25,27,29,31},{33,35,37,39},{41,43..., dimensions={0} | all-to-all | bytes 557056 | tf_op jit(solution)/shard_map/all_to_all | solution.py:244
  71.1 1.2 shard_map.57
  72.2 6.7 %all_to_all.55.recv_ref = f32[4,8,256]{2,1,0:T(8,128)S(1)} all-to-all(f32[4,8,256]{2,1,0:T(8,128)S(1)} %get-tuple-element.42), channel_id=1, replica_groups={{1,129,257,385},{9,137,265,393},{17,145,273,401},{25,153,281,409},{33,1..., dimensions={0} | all-to-all | bytes 65536 | tf_op jit(solution)/shard_map/all_to_all | solution.py:244
  78.9 15.8 %all_to_all.56.recv_ref = f32[16,8,256]{2,1,0:T(8,128)S(1)} all-to-all(f32[16,8,256]{2,1,0:T(8,128)S(1)} %shard_map.58), channel_id=1, replica_groups={{1,9,17,25,33,41,49,57,65,73,81,89,97,105,113,121},{3,11,19,27,35,43,51..., dimensions={0} | all-to-all | bytes 262144 | tf_op jit(solution)/shard_map/all_to_all | solution.py:244
  94.7 7.1 %all_to_all.57.recv_ref = f32[4,8,256]{2,1,0:T(8,128)S(1)} all-to-all(f32[4,8,256]{2,1,0:T(8,128)S(1)} %shard_map.59), channel_id=1, replica_groups={{1,129,257,385},{9,137,265,393},{17,145,273,401},{25,153,281,409},{33,1..., dimensions={0} | all-to-all | bytes 65536 | tf_op jit(solution)/shard_map/all_to_all | solution.py:244
  101.8 2.3 %shard_map.60 = (f32[8,1024]{1,0:T(8,128)S(1)}, f32[4,8,2176]{2,1,0:T(8,128)S(1)}) custom-call(f32[4,8,256]{2,1,0:T(8,128)S(1)} %all_to_all.57.recv_ref, f32[8,1024]{1,0:T(8,128)S(1)} %get-tuple-element.43.resid_ref, bf16[2048,512]{1,0:T(8,128)(2,1)S(1)} %get-tuple-element.38.high0, bf16[2048,512]{1,0:T(8,128)(2,1)S(1)} %get-tuple-element.39.low0, ...), custom_call_target="tpu_custom_call" | custom-call | tf_op jit(solution)/shard_map/pallas_call | solution.py:217
  104.1 8.0 %all_to_all.58.recv_ref = f32[4,8,2176]{2,1,0:T(8,128)S(1)} all-to-all(f32[4,8,2176]{2,1,0:T(8,128)S(1)} %get-tuple-element.44), channel_id=1, replica_groups={{1,3,5,7},{9,11,13,15},{17,19,21,23},{25,27,29,31},{33,35,37,39},{41,43..., dimensions={0} | all-to-all | bytes 557056 | tf_op jit(solution)/shard_map/all_to_all | solution.py:244
  112.1 0.2 shard_map.61
  112.3 18.2 %all_to_all.59.curvature_ref = f32[64,1,128]{2,1,0:T(1,128)S(1)} all-to-all(f32[64,1,128]{2,1,0:T(1,128)S(1)} %get-tuple-element.47), channel_id=1, replica_groups={{1,9,17,25,33,41,49,57,65,73,81,89,97,105,113,121,129,137,145,153,161,1..., dimensions={0} | all-to-all | bytes 65536 | tf_op jit(solution)/shard_map/all_to_all | solution.py:244
  130.5 0.1 shard_map.62
  130.7 1.9 %all-gather.1 = f32[16,3072]{1,0:T(8,128)S(1)} all-gather(f32[8,3072]{1,0:T(8,128)S(1)} %shard_map.62), channel_id=3, replica_groups=mesh['x'=4,'z'=16,'y'=4,'core'=2] {'core'}, dimensions={0}, use_global_device_ids=true | all-gather | bytes 294912 | tf_op jit(solution)/shard_map/all_gather | solution.py:313
  132.6 0.6 shard_map.63
  (5 shorter events, 0.1 us)
Async XLA Ops:
  0.6 20.7 %copy-start = (s32[2048]{0:T(1024)S(1)}, s32[2048]{0:T(1024)}, u32[]{:S(2)}) copy-start(s32[2048]{0:T(1024)} %param.4) | copy-start | bytes 24580
  12.1 9.9 %collective-permute-start = (f32[2048,512]{1,0:T(8,128)S(1)}, f32[2048,512]{1,0:T(8,128)S(1)}, u32[]{:S(2)}, u32[]{:S(2)}) collective-permute-start(f32[2048,512]{1,0:T(8,128)S(1)} %get-tuple-element.35), channel_id=1, source_target_pairs={{0,1},{2,3},{4,5},{6,7},{8,9},{10,11},{12,13},{14,15},{16,17},{18,... | collective-permute-start | bytes 12582920 | tf_op jit(solution)/shard_map/ppermute | solution.py:284
